TPU v7x, 16 devices: a whole 2x2x2 slice. The times are simulated.
16 devices in a mesh: ep: 16 (over z, y, x, core).
Axes of the slice: x: 2, y: 2, z: 2, core: 2. Of those that a mesh axis runs over, the one named last changes fastest.
Arguments:
- tokens: bfloat16 [16, 256, 768], P('ep')
- loss_weight: bfloat16 [16, 256, 768], P('ep')
- w_gate: bfloat16 [768, 16], replicated
- w_in: bfloat16 [16, 768, 3072], P('ep')
- w_out: bfloat16 [16, 3072, 768], P('ep')
- first_expert: int32 [16, 256], P('ep')
- second_expert: int32 [16, 256], P('ep')
- keep_second: int32 [16, 256], P('ep')
Outputs:
- output 1: float32 [], replicated
- output 2: bfloat16 [16, 256, 768], P('ep')
- output 3: bfloat16 [16, 768, 3072], P('ep')
- output 4: bfloat16 [16, 3072, 768], P('ep')
- output 5: float32 [768, 16], replicated
All inputs are finite; a program needn't handle non-finite values.
Results may differ from a plain program's by a relative error of at most 0.00963735.
Values are sent between devices in bfloat16 or wider.
A program may use at most 1 GiB of HBM per device.

v0:
```python
import jax
import jax.numpy as jnp
from jax import lax
from jax.sharding import PartitionSpec as P

ALPHA = 0.01


def gelu_bf16(pre_act):
    return jax.nn.gelu(pre_act, approximate=True).astype(jnp.bfloat16)


def route_masks(first_ids, second_ids, keep_ids, experts, cap_rows):
    seq_len = first_ids.shape[1]
    expert_ids = jnp.arange(experts, dtype=jnp.int32)
    first_hot = (first_ids[..., None] == expert_ids).astype(jnp.bfloat16)
    second_hot = (second_ids[..., None] == expert_ids).astype(jnp.bfloat16)
    second_kept = second_hot * keep_ids.astype(jnp.bfloat16)[..., None]
    seq_ids = jnp.arange(seq_len, dtype=jnp.int32)
    earlier = (seq_ids[:, None] > seq_ids[None, :]).astype(jnp.bfloat16)
    before_first = jnp.einsum('st,gte->gse', earlier, first_hot, preferred_element_type=jnp.float32)
    before_second = jnp.einsum('st,gte->gse', earlier, second_kept, preferred_element_type=jnp.float32)
    first_count = jnp.sum(first_hot, axis=1, dtype=jnp.float32)
    pos_first = jnp.sum(before_first * first_hot, axis=-1)
    pos_second = jnp.sum((before_second + first_count[:, None, :]) * second_hot, axis=-1)
    slot_ids = jnp.arange(cap_rows, dtype=jnp.float32)
    disp_first = first_hot[..., None] * (pos_first[..., None, None] == slot_ids).astype(jnp.bfloat16)
    disp_second = second_kept[..., None] * (pos_second[..., None, None] == slot_ids).astype(jnp.bfloat16)
    return first_hot, second_hot, first_count, disp_first, disp_second


def solution(mesh):
    ep_size = mesh.shape['ep']

    def layer_body(x_loc, r_loc, w_gate, w_in_loc, w_out_loc, first_ids, second_ids, keep_ids):
        local_groups, seq_len, hidden = x_loc.shape
        experts = w_gate.shape[1]
        cap_rows = 2 * seq_len // experts
        tokens_all = local_groups * ep_size * seq_len
        numel = tokens_all * hidden
        first_hot, second_hot, first_count, disp_first, disp_second = route_masks(first_ids, second_ids, keep_ids, experts, cap_rows)
        logits = jnp.einsum('gsh,he->gse', x_loc, w_gate, preferred_element_type=jnp.float32)
        router_prob = jax.nn.softmax(logits, axis=-1)
        gate_first = jnp.sum(router_prob * first_hot, axis=-1)
        gate_second = jnp.sum(router_prob * second_hot, axis=-1)
        gate_sum = gate_first + gate_second
        norm_first = (gate_first / gate_sum).astype(jnp.bfloat16)
        norm_second = (gate_second / gate_sum).astype(jnp.bfloat16)
        dispatch = disp_first + disp_second
        combine = disp_first * norm_first[..., None, None] + disp_second * norm_second[..., None, None]
        send_x = jnp.einsum('gsec,gsh->egch', dispatch, x_loc, preferred_element_type=jnp.float32).astype(jnp.bfloat16)
        expert_x = lax.all_to_all(send_x, 'ep', 0, 1, tiled=True)
        pre_act = jnp.einsum('egch,ehf->egcf', expert_x, w_in_loc, preferred_element_type=jnp.float32)
        act_bf, act_pull = jax.vjp(gelu_bf16, pre_act)
        expert_y = jnp.einsum('egcf,efh->egch', act_bf, w_out_loc, preferred_element_type=jnp.float32).astype(jnp.bfloat16)
        back_y = lax.all_to_all(expert_y, 'ep', 1, 0, tiled=True)
        out_first = jnp.einsum('gsec,egch->gsh', disp_first, back_y, preferred_element_type=jnp.float32).astype(jnp.bfloat16)
        out_second = jnp.einsum('gsec,egch->gsh', disp_second, back_y, preferred_element_type=jnp.float32).astype(jnp.bfloat16)
        moe_out = norm_first.astype(jnp.float32)[..., None] * out_first + norm_second.astype(jnp.float32)[..., None] * out_second
        dot_sum = jnp.einsum('gsh,gsh->', x_loc, r_loc, preferred_element_type=jnp.float32) + jnp.sum(moe_out * r_loc)
        local_stats = jnp.concatenate([jnp.sum(first_count, axis=0), jnp.sum(router_prob, axis=(0, 1)), dot_sum[None]])
        global_stats = lax.psum(local_stats, 'ep')
        frac_first = global_stats[:experts] / tokens_all
        mean_prob = global_stats[experts:2 * experts] / tokens_all
        loss_value = global_stats[2 * experts] / numel + ALPHA * experts * jnp.sum(frac_first * mean_prob)

        grad_send = jnp.einsum('gsec,gsh->egch', combine, r_loc, preferred_element_type=jnp.float32).astype(jnp.bfloat16)
        grad_y = lax.all_to_all(grad_send, 'ep', 0, 1, tiled=True)
        grad_w_out = jnp.einsum('egcf,egch->efh', act_bf, grad_y, preferred_element_type=jnp.float32).astype(jnp.bfloat16)
        grad_act = jnp.einsum('egch,efh->egcf', grad_y, w_out_loc, preferred_element_type=jnp.float32).astype(jnp.bfloat16)
        grad_pre = act_pull(grad_act)[0].astype(jnp.bfloat16)
        grad_w_in = jnp.einsum('egch,egcf->ehf', expert_x, grad_pre, preferred_element_type=jnp.float32).astype(jnp.bfloat16)
        grad_slots = jnp.einsum('egcf,ehf->egch', grad_pre, w_in_loc, preferred_element_type=jnp.float32).astype(jnp.bfloat16)
        grad_back = lax.all_to_all(grad_slots, 'ep', 1, 0, tiled=True)
        grad_x_moe = jnp.einsum('gsec,egch->gsh', dispatch, grad_back, preferred_element_type=jnp.float32)
        grad_norm_first = jnp.einsum('gsh,gsh->gs', r_loc, out_first, preferred_element_type=jnp.float32).astype(jnp.bfloat16).astype(jnp.float32)
        grad_norm_second = jnp.einsum('gsh,gsh->gs', r_loc, out_second, preferred_element_type=jnp.float32).astype(jnp.bfloat16).astype(jnp.float32)
        gate_sq = gate_sum * gate_sum
        grad_gate_first = (grad_norm_first - grad_norm_second) * gate_second / gate_sq
        grad_gate_second = (grad_norm_second - grad_norm_first) * gate_first / gate_sq
        grad_prob = grad_gate_first[..., None] * first_hot + grad_gate_second[..., None] * second_hot + (ALPHA * hidden * experts) * frac_first
        grad_logits = router_prob * (grad_prob - jnp.sum(router_prob * grad_prob, axis=-1, keepdims=True))
        grad_logits_bf = grad_logits.astype(jnp.bfloat16)
        grad_x_router = jnp.einsum('gse,he->gsh', grad_logits_bf, w_gate, preferred_element_type=jnp.float32)
        grad_x = (r_loc.astype(jnp.float32) + grad_x_moe + grad_x_router).astype(jnp.bfloat16)
        grad_gate_w = lax.psum(jnp.einsum('gsh,gse->he', x_loc, grad_logits_bf, preferred_element_type=jnp.float32), 'ep')
        return loss_value, grad_x, grad_w_in, grad_w_out, grad_gate_w

    row_spec = P('ep', None, None)
    id_spec = P('ep', None)
    return jax.shard_map(layer_body, mesh=mesh, in_specs=(row_spec, row_spec, P(None, None), row_spec, row_spec, id_spec, id_spec, id_spec), out_specs=(P(), row_spec, row_spec, row_spec, P(None, None)), check_vma=False)
```

profile of v0, /device:TPU:0, one launch (start us, length us, event | category | flops | bytes accessed | tf_op | source)
XLA Modules:
  0.0 169.4 jit_solution(3151211008225738021)
XLA Ops:
  0.6 0.0 copy-start
  0.6 0.8 convert_reduce_fusion
  1.4 1.0 fusion.50
  2.4 0.7 fusion.98
  3.1 0.7 convert_reduce_fusion.1
  3.8 0.7 fusion.96
  4.5 1.0 fusion.51
  5.5 1.4 fusion.37
  6.8 0.0 slice-start
  6.8 18.4 %all_to_all.16 = bf16[16,1,32,768]{3,2,1,0:T(8,128)(2,1)S(1)} all-to-all(bf16[16,1,32,768]{3,2,1,0:T(8,128)(2,1)S(1)} %fusion.37), channel_id=1, replica_groups=mesh['ep'=16] {'ep'}, dimensions={0} | all-to-all | bytes 1572864 | tf_op jit(solution)/shard_map/all_to_all | solution.py:52
  25.3 4.5 %fusion.16 = f32[16,32,3072]{2,1,0:T(8,128)S(1)} fusion(bf16[1,768,3072]{2,1,0:T(8,128)(2,1)} %param.11, bf16[16,1,32,768]{3,2,1,0:T(8,128)(2,1)S(1)} %all_to_all.16), kind=kOutput, calls=%fused_computation.23 | convolution fusion | flops 2415919104 | bytes 11796480 | tf_op jit(solution)/shard_map/egch,ehf->egcf/dot_general | solution.py:53
  29.8 0.0 copy-start.1
  29.8 2.7 %copy-done.1 = f32[16,32,3072]{2,1,0:T(8,128)} copy-done((f32[16,32,3072]{2,1,0:T(8,128)}, f32[16,32,3072]{2,1,0:T(8,128)S(1)}, u32[]{:S(2)}) %copy-start.1) | copy-done | bytes 6291480
  32.5 0.0 copy-start.5
  32.5 0.0 copy-start.6
  32.5 0.0 copy-start.3
  32.5 4.7 %fusion.31 = bf16[1,16,32,768]{3,2,0,1:T(8,128)(2,1)} fusion(bf16[1,3072,768]{2,1,0:T(8,128)(2,1)S(1)} %bitcast.175, f32[16,32,3072]{2,1,0:T(8,128)S(1)} %fusion.16), kind=kOutput, calls=%fused_computation.32 | convolution fusion | flops 2430468096 | bytes 11796480 | tf_op jit(solution)/shard_map/egcf,efh->egch/dot_general | solution.py:55
  37.2 2.4 %all-to-all-start.1 = ((bf16[1,16,32,768]{3,2,0,1:T(8,128)(2,1)}), bf16[1,16,32,768]{3,2,0,1:T(8,128)(2,1)S(1)}, u32[]{:S(2)}, u32[]{:S(2)}) async-start(bf16[1,16,32,768]{3,2,0,1:T(8,128)(2,1)} %fusion.31), calls=%async_computation.1 | async-start | bytes 1572864 | tf_op jit(solution)/shard_map/all_to_all | solution.py:56
  39.6 0.3 fusion.115
  39.9 0.1 fusion.112
  40.1 0.8 fusion.62
  40.9 12.0 %all-to-all-done.1 = bf16[1,16,32,768]{3,2,0,1:T(8,128)(2,1)S(1)} async-done(((bf16[1,16,32,768]{3,2,0,1:T(8,128)(2,1)}), bf16[1,16,32,768]{3,2,0,1:T(8,128)(2,1)S(1)}, u32[]{:S(2)}, u32[]{:S(2)}) %all-to-all-start.1) | async-done | bytes 786464 | tf_op jit(solution)/shard_map/all_to_all | solution.py:56
  52.9 0.9 copy-done.4
  53.7 0.4 fusion.44
  54.1 1.7 fusion.53
  55.8 1.3 fusion.38
  57.1 3.0 %all-to-all-start.2 = ((bf16[16,1,32,768]{3,2,1,0:T(8,128)(2,1)}), bf16[16,1,32,768]{3,2,1,0:T(8,128)(2,1)}, u32[]{:S(2)}, u32[]{:S(2)}) async-start(bf16[16,1,32,768]{3,2,1,0:T(8,128)(2,1)} %fusion.38), calls=%async_computation.2 | async-start | bytes 1572864 | tf_op jit(solution)/shard_map/all_to_all | solution.py:68
  60.1 1.0 fusion.52
  62.4 0.1 pad_maximum_fusion
  62.5 34.8 %psum.14 = f32[33]{0:T(128)S(1)} all-reduce(f32[33]{0:T(128)S(1)} %pad_maximum_fusion), channel_id=1, replica_groups=mesh['ep'=16] {'ep'}, use_global_device_ids=true, to_apply=%region_9.0 | all-reduce | flops 33 | bytes 264 | tf_op jit(solution)/shard_map/psum | solution.py:62
  97.3 0.6 slice.9
  98.5 0.7 slice_multiply_fusion
  99.9 0.1 multiply_reduce_fusion
  100.0 0.2 convolution_bitcast_fusion.4
  100.2 33.7 %psum.15 = f32[768,16]{0,1:T(8,128)} all-reduce(f32[768,16]{0,1:T(8,128)S(1)} %convolution_bitcast_fusion.4), channel_id=1, replica_groups=mesh['ep'=16] {'ep'}, use_global_device_ids=true, to_apply=%region_12.0 | all-reduce | flops 12288 | bytes 98304 | tf_op jit(solution)/shard_map/psum | solution.py:86
  133.9 0.0 all-to-all-done.2
  133.9 8.6 %fusion.2 = bf16[16,32,3072]{2,1,0:T(8,128)(2,1)S(1)} fusion(f32[16,32,3072]{2,1,0:T(8,128)} %copy-done.1, bf16[1,3072,768]{2,1,0:T(8,128)(2,1)} %param.12, bf16[16,1,32,768]{3,2,1,0:T(8,128)(2,1)} %all-to-all-done.2), kind=kOutput, calls=%fused_computation.8 | convolution fusion | flops 2450522112 | bytes 14942208 | tf_op jit(solution)/shard_map/egch,efh->egcf/dot_general | solution.py:70
  142.5 0.0 copy-start.7
  142.5 1.7 copy-done.7
  144.2 5.8 %fusion.34 = bf16[1,16,32,768]{3,2,0,1:T(8,128)(2,1)} fusion(bf16[16,32,3072]{2,1,0:T(8,128)(2,1)S(1)} %fusion.2, bf16[1,768,3072]{2,1,0:T(8,128)(2,1)} %param.11), kind=kOutput, calls=%fused_computation.33 | convolution fusion | flops 2416312320 | bytes 8650752 | tf_op jit(solution)/shard_map/egcf,ehf->egch/dot_general | solution.py:73
  150.0 3.3 %all-to-all-start.3 = ((bf16[1,16,32,768]{3,2,0,1:T(8,128)(2,1)}), bf16[1,16,32,768]{3,2,0,1:T(8,128)(2,1)S(1)}, u32[]{:S(2)}, u32[]{:S(2)}) async-start(bf16[1,16,32,768]{3,2,0,1:T(8,128)(2,1)} %fusion.34), calls=%async_computation.3 | async-start | bytes 1572864 | tf_op jit(solution)/shard_map/all_to_all | solution.py:74
  153.3 0.0 copy-start.8
  153.3 8.6 %fusion.19 = bf16[1,3072,768]{2,1,0:T(8,128)(2,1)} fusion(bf16[16,1,32,768]{3,2,1,0:T(8,128)(2,1)} %all-to-all-done.2, f32[16,32,3072]{2,1,0:T(8,128)} %copy-done.1), kind=kOutput, calls=%fused_computation.26 | convolution fusion | flops 2432434176 | bytes 11796480 | tf_op jit(solution)/shard_map/egcf,egch->efh/dot_general | solution.py:69
  161.9 0.0 copy-done.8
  161.9 4.3 %fusion.18 = bf16[1,768,3072]{2,1,0:T(8,128)(2,1)} fusion(bf16[16,32,3072]{2,1,0:T(8,128)(2,1)S(1)} %copy-done.8, bf16[16,1,32,768]{3,2,1,0:T(8,128)(2,1)S(1)} %all_to_all.16), kind=kOutput, calls=%fused_computation.25 | convolution fusion | flops 2418278400 | bytes 8650752 | tf_op jit(solution)/shard_map/egch,egcf->ehf/dot_general | solution.py:72
  166.2 0.5 all-to-all-done.3
  166.7 0.4 fusion.40
  167.1 1.1 fusion.45
  (14 shorter events, 0.1 us)
Async XLA Ops:
  0.6 39.0 %copy-start = (bf16[768,16]{0,1:T(8,128)(2,1)S(1)}, bf16[768,16]{0,1:T(8,128)(2,1)}, u32[]{:S(2)}) copy-start(bf16[768,16]{0,1:T(8,128)(2,1)} %param.10) | copy-start | bytes 73732
  6.8 25.6 %slice-start = ((s8[4718592]{0:T(1024)(128)(4,1)}), s8[4194304]{0:T(1024)(128)(4,1)S(1)}, s32[]{:S(2)}) async-start(s8[4718592]{0:T(1024)(128)(4,1)} %bitcast.174), calls=%async_computation.4 | async-start | bytes 8388608
  25.3 7.2 %slice-start.1 = ((s8[4718592]{0:T(1024)(128)(4,1)}), s8[524288]{0:T(1024)(128)(4,1)S(1)}, s32[]{:S(2)}) async-start(s8[4718592]{0:T(1024)(128)(4,1)} %bitcast.174), calls=%async_computation.5 | async-start | bytes 1048576
  29.8 2.7 %copy-start.1 = (f32[16,32,3072]{2,1,0:T(8,128)}, f32[16,32,3072]{2,1,0:T(8,128)S(1)}, u32[]{:S(2)}) copy-start(f32[16,32,3072]{2,1,0:T(8,128)S(1)} %fusion.16) | copy-start | bytes 18874372
  32.5 7.1 %copy-start.2 = (bf16[1,256,768]{2,1,0:T(8,128)(2,1)S(1)}, bf16[1,256,768]{2,1,0:T(8,128)(2,1)}, u32[]{:S(2)}) copy-start(bf16[1,256,768]{2,1,0:T(8,128)(2,1)} %param.8) | copy-start | bytes 1179652
  32.5 7.4 %copy-start.5 = (s32[1,256]{1,0:T(1,128)S(1)}, s32[1,256]{1,0:T(1,128)}, u32[]{:S(2)}) copy-start(s32[1,256]{1,0:T(1,128)} %param.13) | copy-start | bytes 3076
  32.5 7.4 %copy-start.6 = (s32[1,256]{1,0:T(1,128)S(1)}, s32[1,256]{1,0:T(1,128)}, u32[]{:S(2)}) copy-start(s32[1,256]{1,0:T(1,128)} %param.14) | copy-start | bytes 3076
  32.5 7.6 %copy-start.3 = (bf16[1,256,768]{2,1,0:T(8,128)(2,1)S(1)}, bf16[1,256,768]{2,1,0:T(8,128)(2,1)}, u32[]{:S(2)}) copy-start(bf16[1,256,768]{2,1,0:T(8,128)(2,1)} %param.9) | copy-start | bytes 1179652
  37.2 15.6 %all-to-all-start.1 = ((bf16[1,16,32,768]{3,2,0,1:T(8,128)(2,1)}), bf16[1,16,32,768]{3,2,0,1:T(8,128)(2,1)S(1)}, u32[]{:S(2)}, u32[]{:S(2)}) async-start(bf16[1,16,32,768]{3,2,0,1:T(8,128)(2,1)} %fusion.31), calls=%async_computation.1 | async-start | bytes 1572864 | tf_op jit(solution)/shard_map/all_to_all | solution.py:56
  52.9 0.9 copy-start.4
  57.1 76.8 %all-to-all-start.2 = ((bf16[16,1,32,768]{3,2,1,0:T(8,128)(2,1)}), bf16[16,1,32,768]{3,2,1,0:T(8,128)(2,1)}, u32[]{:S(2)}, u32[]{:S(2)}) async-start(bf16[16,1,32,768]{3,2,1,0:T(8,128)(2,1)} %fusion.38), calls=%async_computation.2 | async-start | bytes 1572864 | tf_op jit(solution)/shard_map/all_to_all | solution.py:68
  142.5 1.7 copy-start.7
  150.0 16.7 %all-to-all-start.3 = ((bf16[1,16,32,768]{3,2,0,1:T(8,128)(2,1)}), bf16[1,16,32,768]{3,2,0,1:T(8,128)(2,1)S(1)}, u32[]{:S(2)}, u32[]{:S(2)}) async-start(bf16[1,16,32,768]{3,2,0,1:T(8,128)(2,1)} %fusion.34), calls=%async_computation.3 | async-start | bytes 1572864 | tf_op jit(solution)/shard_map/all_to_all | solution.py:74
  153.3 8.6 %copy-start.8 = (bf16[16,32,3072]{2,1,0:T(8,128)(2,1)S(1)}, bf16[16,32,3072]{2,1,0:T(8,128)(2,1)}, u32[]{:S(2)}) copy-start(bf16[16,32,3072]{2,1,0:T(8,128)(2,1)} %copy-done.7) | copy-start | bytes 9437188
where the time goes:
time: 170 us; the launch traced here: 169 us
  blocking collectives  87 us (51%)
  matrix products  45.2 us (27%)
  waiting for transfers between devices  12.5 us (7%)
  starting transfers between devices  8.67 us (5%)
  local copies, waits for them, and re-layouts  5.82 us (3%)
  other arithmetic  5.68 us (3%)
  between operations  4.56 us (3%)
    psum x1, blocking collectives, layer_body(): global_stats = lax.psum(local_stats, 'ep')  34.8 us
    psum x1, blocking collectives, layer_body(): lax.psum(jnp.einsum('gsh,gse->he', x_loc, grad_logits_bf, preferred_eleme...  33.7 us
    all_to_all x1, blocking collectives, layer_body(): expert_x = lax.all_to_all(send_x, 'ep', 0, 1, tiled=True)  18.4 us
    all_to_all x1, waiting for transfers between devices, layer_body(): back_y = lax.all_to_all(expert_y, 'ep', 1, 0, tiled=True)  12 us
    dot_general x1, matrix products, layer_body(): jnp.einsum('egcf,egch->efh', act_bf, grad_y, preferred_element_type=jnp.f...  8.6 us
    dot_general x1, matrix products, layer_body(): jnp.einsum('egch,efh->egcf', grad_y, w_out_loc, preferred_element_type=jn...  8.59 us
    dot_general x1, matrix products, layer_body(): jnp.einsum('egcf,ehf->egch', grad_pre, w_in_loc, preferred_element_type=j...  5.85 us
    unnamed x22, local copies, waits for them, and re-layouts  5.24 us
  transfers between devices with their start and end apart: 3, of which 2 were waited for; matrix products, arithmetic and copies ran while one was open for 10% of the time, Pallas kernels for 0%

commit v1 on v0

v1 whole, which is shorter than its diff:
```python
import functools

import jax
import jax.numpy as jnp
from jax import lax
from jax.experimental import pallas as pl
from jax.experimental.pallas import tpu as pltpu
from jax.sharding import PartitionSpec as P

ALPHA = 0.01
MESH = pl.DeviceIdType.MESH
F32 = jnp.float32
BF16 = jnp.bfloat16

DEVS = 16
LANES = 128
PAD = 8
HALF = 8

SEND_X, SEND_R, SEND_MSG, SEND_DOT, SEND_GX, SEND_RS, SEND_AG = range(7)


def offset_of(p):
    x, y = (p >> 1) & 1, (p >> 2) & 1
    z = x ^ y ^ ((p >> 3) & 1)
    return (p & 1) | (x << 1) | (y << 2) | (z << 3)


def block_of(ids, me):
    k = jnp.bitwise_xor(ids, me)
    parity = (k >> 1) ^ (k >> 2) ^ (k >> 3)
    return (k & 7) + 8 * (parity & 1)


def dot(a, b, ca=1, cb=0):
    return lax.dot_general(a, b, (((ca,), (cb,)), ((), ())), preferred_element_type=F32)


def iota(shape, axis):
    return lax.broadcasted_iota(jnp.int32, shape, axis)


def where(mask, value):
    return jnp.where(mask, value, jnp.zeros_like(value))


def tree_sum(rows):
    rows = list(rows)
    while len(rows) > 1:
        rows = [rows[i] + rows[i + 1] for i in range(0, len(rows), 2)]
    return rows[0]


def rows_of(ref, n, width=LANES):
    out = jnp.zeros((n, width), F32)
    sub = iota((n, width), 0)
    for i in range(n):
        out = jnp.where(sub == i, jnp.broadcast_to(ref[i], (n, width)), out)
    return out


def layer_kernel(cap, x_hbm, r_hbm, wg_hbm, w1_hbm, w2_hbm, e1_hbm, e2_hbm, k2_hbm,
                 loss_ref, gx_ref, dw1_ref, dw2_ref, gw_ref,
                 x, r, wg, w1, w2, ids, disp, xs, rs, xe, re, gy, act, slope, dpre, ybuf, gxs, gxb, xet,
                 msg_s, msg_r, dot_s, dot_r, red_s, red_r, row_s, row_r,
                 local_sem, send_sem, recv_sem):
    seq, hidden = x.shape
    ff = w1.shape[1]
    half = HALF * cap
    tokens_all = DEVS * seq
    numel = tokens_all * hidden

    me = lax.axis_index("ep")
    bits = [lax.rem(me // (1 << i), 2) for i in range(4)]

    def peer(p):
        k = offset_of(p)
        return sum(((1 - bits[i]) if (k >> i) & 1 else bits[i]) * (1 << i) for i in range(4))

    def remote(kind, p, src, dst):
        return pltpu.make_async_remote_copy(
            src_ref=src, dst_ref=dst, send_sem=send_sem.at[kind, p], recv_sem=recv_sem.at[kind, p],
            device_id=(peer(p),), device_id_type=MESH)

    others = range(1, DEVS)

    loads = [pltpu.make_async_copy(src, dst, local_sem.at[i]) for i, (src, dst) in enumerate((
        (e1_hbm, ids.at[0]), (e2_hbm, ids.at[1]), (k2_hbm, ids.at[2]), (x_hbm, x), (r_hbm, r),
        (wg_hbm, wg), (w1_hbm, w1), (w2_hbm, w2)))]
    for copy in loads:
        copy.start()
    barrier = pltpu.get_barrier_semaphore()
    for p in others:
        pl.semaphore_signal(barrier, inc=1, device_id=(peer(p),), device_id_type=MESH)

    for i in range(3):
        loads[i].wait()
    e1, e2, k2 = ids[0], ids[1], ids[2]
    expert = iota((DEVS, seq), 0)
    hot1 = (e1 == expert).astype(F32)
    hot2 = (e2 == expert).astype(F32)
    kept2 = hot2 * k2.astype(F32)
    earlier = (iota((seq, seq), 0) < iota((seq, seq), 1)).astype(F32).astype(BF16)
    before = dot(jnp.concatenate([hot1, kept2], axis=0).astype(BF16), earlier)
    count1 = jnp.sum(hot1, axis=1, keepdims=True)
    pos1 = jnp.sum(before[:DEVS] * hot1, axis=0, keepdims=True).astype(jnp.int32)
    pos2 = jnp.sum((before[DEVS:] + count1) * hot2, axis=0, keepdims=True).astype(jnp.int32)
    keep1 = pos1 < cap
    keep2 = (pos2 < cap) & (k2 > 0)
    block1, block2 = block_of(e1, me), block_of(e2, me)
    slot1 = jnp.where(keep1, block1 * cap + pos1, -1)
    slot2 = jnp.where(keep2, block2 * cap + pos2, -1)

    loads[3].wait()
    for c in range(2):
        rows = pl.ds(c * half, half)
        slot = iota((half, seq), 0) + c * half
        table = ((slot == slot1) | (slot == slot2)).astype(F32).astype(BF16)
        disp[rows, :] = table
        xs[rows, :] = dot(table, x[...]).astype(BF16)
    pl.semaphore_wait(barrier, DEVS - 1)
    blk = lambda ref, p: ref.at[pl.ds(p * cap, cap), :]
    copies_x = {p: remote(SEND_X, p, blk(xs, p), blk(xe, p)) for p in others}
    for p in others:
        copies_x[p].start()
    xe[pl.ds(0, cap), :] = xs[pl.ds(0, cap), :]

    loads[4].wait()
    for c in range(2):
        rows = pl.ds(c * half, half)
        rs[rows, :] = dot(disp[rows, :], r[...]).astype(BF16)
    loads[5].wait()
    logits = dot(wg[...], x[...], 1, 1)
    shifted = jnp.exp(logits - jnp.max(logits, axis=0, keepdims=True))
    prob = shifted / jnp.sum(shifted, axis=0, keepdims=True)
    gate1 = jnp.sum(prob * hot1, axis=0, keepdims=True)
    gate2 = jnp.sum(prob * hot2, axis=0, keepdims=True)
    gate_sum = gate1 + gate2
    norm1 = (gate1 / gate_sum).astype(BF16).astype(F32)
    norm2 = (gate2 / gate_sum).astype(BF16).astype(F32)
    place = iota((LANES, seq), 0)
    at1 = (place == jnp.where(keep1, pos1, -1)).astype(F32).astype(BF16)
    at2 = (place == jnp.where(keep2, pos2, -1)).astype(F32).astype(BF16)
    weights = dot((hot1 * norm1).astype(BF16), at1, 1, 1) + dot((hot2 * norm2).astype(BF16), at2, 1, 1)
    prob_sum = jnp.sum(prob, axis=1, keepdims=True)
    sub, lane = iota((DEVS, LANES), 0), iota((DEVS, LANES), 1)
    stats = where(lane == sub + cap, jnp.broadcast_to(count1, (DEVS, LANES)))
    stats += where(lane == sub + cap + DEVS, jnp.broadcast_to(prob_sum, (DEVS, LANES)))
    message = weights + jnp.sum(stats, axis=0, keepdims=True)
    for e in range(DEVS):
        msg_s[e] = message[e:e + 1]
    msg_r[0] = msg_s[me]
    copies_msg = {p: remote(SEND_MSG, p, msg_s.at[peer(p)], msg_r.at[p]) for p in others}
    copies_r = {p: remote(SEND_R, p, blk(rs, p), blk(re, p)) for p in others}
    for p in others:
        copies_msg[p].start()
    for p in others:
        copies_r[p].start()
    re[pl.ds(0, cap), :] = rs[pl.ds(0, cap), :]

    loads[6].wait()
    loads[7].wait()
    wide = 512
    for c in range(2):
        rows = pl.ds(c * half, half)
        for p in range(c * HALF, (c + 1) * HALF):
            if p:
                copies_x[p].wait_recv()

        @pl.loop(0, ff // wide)
        def _(n):
            cols = pl.ds(pl.multiple_of(n * wide, wide), wide)
            pre = dot(xe[rows, :], w1[:, cols])
            sq = pre * pre
            root = 0.7978845608028654
            t = jnp.tanh(pre * (root + root * 0.044715 * sq))
            hx = 0.5 * pre
            act[rows, cols] = (hx + hx * t).astype(BF16)
            slope[rows, cols] = (0.5 + 0.5 * t) + hx * (1.0 - t * t) * (root + 3.0 * root * 0.044715 * sq)

        @pl.loop(0, hidden // 256)
        def _(n):
            cols = pl.ds(pl.multiple_of(n * 256, 256), 256)
            ybuf[rows, cols] = dot(act[rows, :], w2[:, cols]).astype(BF16)

    copies_dot, copies_gx = {}, {}
    for c in range(2):
        rows = pl.ds(c * half, half)
        mine = range(c * HALF, (c + 1) * HALF)
        for p in mine:
            if p:
                copies_msg[p].wait_recv()
                copies_r[p].wait_recv()
        diag = iota((half, LANES), 1) == lax.rem(iota((half, LANES), 0), cap)
        spread = jnp.concatenate([jnp.broadcast_to(msg_r[p], (cap, LANES)) for p in mine], axis=0)
        weight = jnp.sum(where(diag, spread), axis=1, keepdims=True)
        r_rows = re[rows, :].astype(F32)
        gy[rows, :] = (r_rows * weight).astype(BF16)
        dots = jnp.sum(r_rows * ybuf[rows, :].astype(F32), axis=1, keepdims=True)
        dot_mat = where(diag, jnp.broadcast_to(dots, (half, LANES)))
        for p in mine:
            q = (p - c * HALF) * cap
            row = jnp.sum(dot_mat[q:q + cap], axis=0, keepdims=True)
            if p:
                dot_s[p] = row
            else:
                dot_r[p] = row

        @pl.loop(0, ff // wide)
        def _(n):
            cols = pl.ds(pl.multiple_of(n * wide, wide), wide)
            da = dot(gy[rows, :], w2[cols, :], 1, 1).astype(BF16).astype(F32)
            dpre[rows, cols] = (da * slope[rows, cols]).astype(BF16)

        for p in mine:
            if p:
                copies_dot[p] = remote(SEND_DOT, p, dot_s.at[p], dot_r.at[p])
                copies_dot[p].start()

        @pl.loop(0, hidden // 256)
        def _(n):
            cols = pl.ds(pl.multiple_of(n * 256, 256), 256)
            gxs[rows, cols] = dot(dpre[rows, :], w1[cols, :], 1, 1).astype(BF16)

        xet[:, rows] = jnp.transpose(xe[rows, :])
        for p in mine:
            if p:
                copies_gx[p] = remote(SEND_GX, p, blk(gxs, p), blk(gxb, p))
                copies_gx[p].start()
            else:
                gxb[pl.ds(0, cap), :] = gxs[pl.ds(0, cap), :]

    totals = tree_sum([msg_r[p] for p in range(DEVS)])
    spread = jnp.broadcast_to(totals, (DEVS, LANES))
    count_all = jnp.sum(where(lane == sub + cap, spread), axis=1, keepdims=True)
    prob_all = jnp.sum(where(lane == sub + cap + DEVS, spread), axis=1, keepdims=True)
    frac = count_all * (1.0 / tokens_all)
    for p in others:
        copies_dot[p].wait_recv()
    dots = rows_of(dot_r, DEVS)
    dots_bf = dots.astype(BF16)
    found1 = dot(dots_bf, at1)
    found2 = dot(dots_bf, at2)
    grad1 = jnp.sum(where(block1 == expert, found1), axis=0, keepdims=True)
    grad2 = jnp.sum(where(block2 == expert, found2), axis=0, keepdims=True)
    inv_sq = 1.0 / (gate_sum * gate_sum)
    dgate1 = (grad1 - grad2) * gate2 * inv_sq
    dgate2 = (grad2 - grad1) * gate1 * inv_sq
    dprob = dgate1 * hot1 + dgate2 * hot2 + (ALPHA * hidden * DEVS) * frac
    dlogits = prob * (dprob - jnp.sum(prob * dprob, axis=0, keepdims=True))
    dlog_bf = dlogits.astype(BF16)
    grad_gate = dot(dlog_bf, x[...])
    own = jnp.sum(jnp.sum(x[...].astype(F32) * r[...].astype(F32), axis=0, keepdims=True), axis=1, keepdims=True)
    moe = jnp.sum(norm1 * jnp.sum(where(block1 == expert, dot_f32(dots, at1)), axis=0, keepdims=True)
                  + norm2 * jnp.sum(where(block2 == expert, dot_f32(dots, at2)), axis=0, keepdims=True),
                  axis=1, keepdims=True)
    part = jnp.broadcast_to(own + moe, (DEVS, LANES))
    reduced = jnp.concatenate([grad_gate, part], axis=1)
    for e in range(DEVS):
        red_s[e] = reduced[e:e + 1]
    red_r[0] = red_s[me]
    copies_rs = {p: remote(SEND_RS, p, red_s.at[peer(p)], red_r.at[p]) for p in others}
    for p in others:
        copies_rs[p].start()

    @pl.loop(0, ff // 256)
    def _(n):
        cols = pl.ds(pl.multiple_of(n * 256, 256), 256)
        dw2_ref[cols, :] = dot(act[:, cols], gy[...], 0, 0).astype(BF16)

    for p in others:
        copies_rs[p].wait_recv()
    total = tree_sum([red_r[p] for p in range(DEVS)])
    row_s[0] = total[:, :hidden]
    row_r[me] = total[:, :hidden]
    copies_ag = {p: remote(SEND_AG, p, row_s.at[0], row_r.at[me]) for p in others}
    dot_total = total[:, hidden:hidden + 1]
    aux = DEVS * jnp.sum(frac * (prob_all * (1.0 / tokens_all)), axis=0, keepdims=True)
    loss_ref[...] = jnp.broadcast_to(dot_total * (1.0 / numel) + ALPHA * aux, loss_ref.shape)
    for p in others:
        copies_ag[p].start()

    @pl.loop(0, ff // wide)
    def _(n):
        cols = pl.ds(pl.multiple_of(n * wide, wide), wide)
        dw1_ref[:, cols] = dot(xet[...], dpre[:, cols]).astype(BF16)

    dlog_pad = jnp.concatenate([dlogits, jnp.zeros((LANES - DEVS, seq), F32)], axis=0)
    gate_pad = jnp.concatenate([wg[...], jnp.zeros((LANES - DEVS, hidden), BF16)], axis=0)
    router = dot(jnp.transpose(dlog_pad).astype(BF16), gate_pad)
    base = r[...].astype(F32) + router
    for p in others:
        copies_gx[p].wait_recv()
    gx_ref[...] = (base + dot(disp[...], gxb[...], 0, 0)).astype(BF16)

    for p in others:
        copies_ag[p].wait_recv()
    gw_ref[...] = rows_of(row_r, DEVS, hidden)

    for group in (copies_x, copies_r, copies_msg, copies_dot, copies_gx, copies_rs, copies_ag):
        for p in others:
            group[p].wait_send()


def dot_f32(values, table):
    high = values.astype(BF16)
    rest = values - high.astype(F32)
    mid = rest.astype(BF16)
    low = (rest - mid.astype(F32)).astype(BF16)
    return dot(high, table) + dot(mid, table) + dot(low, table)


def store_kernel(loss, gx, dw1, dw2, gw, loss_out, gx_out, dw1_out, dw2_out, gw_out, sem):
    copies = [pltpu.make_async_copy(src, dst, sem.at[i]) for i, (src, dst) in enumerate((
        (dw1, dw1_out), (dw2, dw2_out), (gx, gx_out), (gw, gw_out)))]
    for copy in copies:
        copy.start()
    loss_out[0, 0] = jnp.max(loss[...])
    for copy in copies:
        copy.wait()


def solution(mesh):
    def layer_body(x_loc, r_loc, w_gate, w_in_loc, w_out_loc, first_ids, second_ids, keep_ids):
        _, seq, hidden = x_loc.shape
        ff = w_in_loc.shape[2]
        cap = 2 * seq // DEVS
        slots = DEVS * cap
        anyspace = pl.BlockSpec(memory_space=pl.ANY)
        vmem = pl.BlockSpec(memory_space=pltpu.VMEM)
        results = pl.pallas_call(
            functools.partial(layer_kernel, cap),
            out_shape=(
                pltpu.VMEM((8, LANES), F32),
                pltpu.VMEM((seq, hidden), BF16),
                pltpu.VMEM((hidden, ff), BF16),
                pltpu.VMEM((ff, hidden), BF16),
                pltpu.VMEM((DEVS, hidden), F32),
            ),
            in_specs=[anyspace] * 8,
            out_specs=(vmem,) * 5,
            scratch_shapes=[
                pltpu.VMEM((seq, hidden), BF16),
                pltpu.VMEM((seq, hidden), BF16),
                pltpu.VMEM((DEVS, hidden), BF16),
                pltpu.VMEM((hidden, ff), BF16),
                pltpu.VMEM((ff, hidden), BF16),
                pltpu.VMEM((3 + PAD, 1, seq), jnp.int32),
                pltpu.VMEM((slots, seq), BF16),
                pltpu.VMEM((slots, hidden), BF16),
                pltpu.VMEM((slots, hidden), BF16),
                pltpu.VMEM((slots, hidden), BF16),
                pltpu.VMEM((slots, hidden), BF16),
                pltpu.VMEM((slots, hidden), BF16),
                pltpu.VMEM((slots, ff), BF16),
                pltpu.VMEM((slots, ff), F32),
                pltpu.VMEM((slots, ff), BF16),
                pltpu.VMEM((slots, hidden), BF16),
                pltpu.VMEM((slots, hidden), BF16),
                pltpu.VMEM((slots, hidden), BF16),
                pltpu.VMEM((hidden, slots), BF16),
                pltpu.VMEM((DEVS + PAD, 1, LANES), F32),
                pltpu.VMEM((DEVS + PAD, 1, LANES), F32),
                pltpu.VMEM((DEVS + PAD, 1, LANES), F32),
                pltpu.VMEM((DEVS + PAD, 1, LANES), F32),
                pltpu.VMEM((DEVS + PAD, 1, hidden + LANES), F32),
                pltpu.VMEM((DEVS + PAD, 1, hidden + LANES), F32),
                pltpu.VMEM((1 + PAD, 1, hidden), F32),
                pltpu.VMEM((DEVS + PAD, 1, hidden), F32),
                pltpu.SemaphoreType.DMA((8,)),
                pltpu.SemaphoreType.DMA((7, DEVS)),
                pltpu.SemaphoreType.DMA((7, DEVS)),
            ],
            compiler_params=pltpu.CompilerParams(
                collective_id=0, has_side_effects=True, vmem_limit_bytes=48 * 1024 * 1024),
            name="moe_layer",
        )(x_loc[0], r_loc[0], w_gate.T, w_in_loc[0], w_out_loc[0], first_ids, second_ids, keep_ids)
        loss, gx, dw1, dw2, gw = pl.pallas_call(
            store_kernel,
            out_shape=(
                jax.ShapeDtypeStruct((1, 1), F32),
                jax.ShapeDtypeStruct((seq, hidden), BF16),
                jax.ShapeDtypeStruct((hidden, ff), BF16),
                jax.ShapeDtypeStruct((ff, hidden), BF16),
                jax.ShapeDtypeStruct((DEVS, hidden), F32),
            ),
            in_specs=[vmem] * 5,
            out_specs=(pl.BlockSpec(memory_space=pltpu.SMEM),) + (anyspace,) * 4,
            scratch_shapes=[pltpu.SemaphoreType.DMA((4,))],
            compiler_params=pltpu.CompilerParams(vmem_limit_bytes=2 * 1024 * 1024),
            name="store_results",
        )(*results)
        return loss.reshape(()), gx[None], dw1[None], dw2[None], gw.T

    row_spec = P('ep', None, None)
    id_spec = P('ep', None)
    return jax.shard_map(layer_body, mesh=mesh, in_specs=(row_spec, row_spec, P(None, None), row_spec, row_spec, id_spec, id_spec, id_spec), out_specs=(P(), row_spec, row_spec, row_spec, P(None, None)), check_vma=False)
```

time: 170 us -> 54.2 us (0.32)
  blocking collectives: 87 us -> 0 us
  Pallas kernels: 0 us -> 53.4 us
  matrix products: 45.2 us -> 0 us
  waiting for transfers between devices: 12.5 us -> 0 us
  starting transfers between devices: 8.67 us -> 0 us
  local copies, waits for them, and re-layouts: 5.82 us -> 0 us
  other arithmetic: 5.68 us -> 0 us
  between operations: 4.56 us -> 0.64 us
    psum x2 -> x0, blocking collectives: 68.6 us -> none  [the longest x1 34.8 us: layer_body(): global_stats = lax.psum(local_stats, 'ep')]
    pallas_call x0 -> x2, Pallas kernels: none -> 53.4 us  [the longest x1 49.1 us: layer_body(): pl.pallas_call(functools.partial(layer_kernel, cap), out_shape=(pltpu.VME...]
    dot_general x16 -> x0, matrix products: 45.2 us -> none  [the longest x1 8.6 us: layer_body(): jnp.einsum('egcf,egch->efh', act_bf, grad_y, preferred_element_type=jnp.f...]
    all_to_all x1 -> x0, blocking collectives: 18.4 us -> none  [layer_body(): expert_x = lax.all_to_all(send_x, 'ep', 0, 1, tiled=True)]
    all_to_all x3 -> x0, waiting for transfers between devices: 12.5 us -> none  [the longest x1 12 us: layer_body(): back_y = lax.all_to_all(expert_y, 'ep', 1, 0, tiled=True)]
    all_to_all x3 -> x0, starting transfers between devices: 8.67 us -> none  [the longest x1 3.29 us: layer_body(): grad_back = lax.all_to_all(grad_slots, 'ep', 1, 0, tiled=True)]
    unnamed x22 -> x0, local copies, waits for them, and re-layouts: 5.24 us -> none
    reduce_sum x5 -> x0, other arithmetic: 2.02 us -> none  [the longest x1 0.98 us: layer_body(): jnp.sum(moe_out * r_loc)]
  transfers between devices with their start and end apart: 3 -> 0, of which waited for: 2 -> 0; matrix products, arithmetic and copies ran while one was open for 10% -> 0% of each run, Pallas kernels for 0% -> 0%
where the time goes in v1:
time: 54.2 us; the launch traced here: 54.1 us
  Pallas kernels  53.4 us (99%)
  between operations  0.64 us (1%)
    pallas_call x1, Pallas kernels, layer_body(): pl.pallas_call(functools.partial(layer_kernel, cap), out_shape=(pltpu.VME...  49.1 us
    pallas_call x1, Pallas kernels, layer_body(): pl.pallas_call(store_kernel, out_shape=(jax.ShapeDtypeStruct((1, 1), F32)...  4.3 us

profile of v1, /device:TPU:0, one launch (start us, length us, event | category | flops | bytes accessed | tf_op | source)
XLA Modules:
  0.0 54.1 jit_solution(18039991067975357053)
XLA Ops:
  0.6 49.1 %moe_layer.1 = (f32[8,128]{1,0:T(8,128)S(1)}, bf16[256,768]{1,0:T(8,128)(2,1)S(1)}, bf16[768,3072]{1,0:T(8,128)(2,1)S(1)}, bf16[3072,768]{1,0:T(8,128)(2,1)S(1)}, f32[16,768]{1,0:T(8,128)S(1)}) custom-call(bf16[256,768]{1,0:T(8,128)(2,1)} %bitcast.12, bf16[256,768]{1,0:T(8,128)(2,1)} %bitcast.13, bf16[16,768]{1,0:T(8,128)(2,1)} %bitcast.14, ...), custom_call_target="tpu_custom_call" | custom-call | tf_op jit(solution)/shard_map/moe_layer/pallas_call | solution.py:331
  49.8 4.3 %store_results.1 = (f32[1,1]{1,0:T(1,128)}, bf16[256,768]{1,0:T(8,128)(2,1)}, bf16[768,3072]{1,0:T(8,128)(2,1)}, bf16[3072,768]{1,0:T(8,128)(2,1)}, f32[16,768]{1,0:T(8,128)}) custom-call(f32[8,128]{1,0:T(8,128)S(1)} %get-tuple-element.15.loss, bf16[256,768]{1,0:T(8,128)(2,1)S(1)} %get-tuple-element.16.gx, bf16[768,3072]{1,0:T(8,128)(2,1)S(1)} %get-tuple-element.17.dw1, ...), custom_call_target="tpu_custom_call" | custom-call | tf_op jit(solution)/shard_map/store_results/pallas_call | solution.py:378

commit v2 on v1

v2 whole, which is shorter than its diff:
```python
import functools

import jax
import jax.numpy as jnp
from jax import lax
from jax.experimental import pallas as pl
from jax.experimental.pallas import tpu as pltpu
from jax.sharding import PartitionSpec as P

ALPHA = 0.01
MESH = pl.DeviceIdType.MESH
F32 = jnp.float32
BF16 = jnp.bfloat16

DEVS = 16
LANES = 128
PAD = 8
HALF = 8

SEND_X, SEND_R, SEND_MSG, SEND_DOT, SEND_GX, SEND_RS, SEND_AG = range(7)


def offset_of(p):
    x, y = (p >> 1) & 1, (p >> 2) & 1
    z = x ^ y ^ ((p >> 3) & 1)
    return (p & 1) | (x << 1) | (y << 2) | (z << 3)


def block_of(ids, me):
    k = jnp.bitwise_xor(ids, me)
    parity = (k >> 1) ^ (k >> 2) ^ (k >> 3)
    return (k & 7) + 8 * (parity & 1)


def dot(a, b, ca=1, cb=0):
    return lax.dot_general(a, b, (((ca,), (cb,)), ((), ())), preferred_element_type=F32)


def iota(shape, axis):
    return lax.broadcasted_iota(jnp.int32, shape, axis)


def where(mask, value):
    return jnp.where(mask, value, jnp.zeros_like(value))


def tree_sum(rows):
    rows = list(rows)
    while len(rows) > 1:
        rows = [rows[i] + rows[i + 1] for i in range(0, len(rows), 2)]
    return rows[0]


def rows_of(ref, places, width):
    n = len(places)
    out = jnp.zeros((n, width), F32)
    sub = iota((n, width), 0)
    for i, place in enumerate(places):
        out = jnp.where(sub == place, jnp.broadcast_to(ref[i], (n, width)), out)
    return out


def split3(values):
    high = values.astype(BF16)
    rest = values - high.astype(F32)
    mid = rest.astype(BF16)
    return high, mid, (rest - mid.astype(F32)).astype(BF16)


def layer_kernel(cap, x_hbm, r_hbm, wg_hbm, w1_hbm, w2_hbm, e1_hbm, e2_hbm, k2_hbm,
                 loss_ref, gx_ref, dw1_ref, dw2_ref, gw_ref,
                 x, r, wg, w1, w2, ids, disp, dispt, xs, rs, xe, re, gy, pre, act, actt, acc, slope, dpre, ybuf, gxs, gxb, xet,
                 msg_s, msg_r, dot_s, dot_r, red_s, red_r, row_s, row_r,
                 local_sem, send_sem, recv_sem):
    seq, hidden = x.shape
    ff = w1.shape[1]
    half = HALF * cap
    tokens_all = DEVS * seq
    numel = tokens_all * hidden

    me = lax.axis_index("ep")
    bits = [lax.rem(me // (1 << i), 2) for i in range(4)]

    def peer(p):
        k = offset_of(p)
        return sum(((1 - bits[i]) if (k >> i) & 1 else bits[i]) * (1 << i) for i in range(4))

    def remote(kind, p, src, dst):
        return pltpu.make_async_remote_copy(
            src_ref=src, dst_ref=dst, send_sem=send_sem.at[kind], recv_sem=recv_sem.at[kind, p // HALF],
            device_id=(peer(p),), device_id_type=MESH)

    others = range(1, DEVS)
    halves = (range(1, HALF), range(HALF, DEVS))
    blk = lambda ref, p, n=1: ref.at[pl.ds(p * cap, n * cap), :]
    row = lambda ref, p, n=1: ref.at[pl.ds(p, n)]

    def wait_half(kind, c, part, ref):
        first, count = halves[c][0], len(halves[c])
        view = part(ref, first, count)
        remote(kind, first, view, view).wait_recv()

    id_copies = [pltpu.make_async_copy(src, ids.at[i], local_sem.at[0]) for i, src in enumerate((e1_hbm, e2_hbm, k2_hbm))]
    id_wait = pltpu.make_async_copy(row(ids, 0, 3), row(ids, 0, 3), local_sem.at[0])
    x_copy, r_copy, wg_copy, w1_copy, w2_copy = [
        pltpu.make_async_copy(src, dst, local_sem.at[1 + i]) for i, (src, dst) in enumerate((
            (x_hbm, x), (r_hbm, r), (wg_hbm, wg), (w1_hbm, w1), (w2_hbm, w2)))]
    barrier = pltpu.get_barrier_semaphore()
    for p in others:
        pl.semaphore_signal(barrier, inc=1, device_id=(peer(p),), device_id_type=MESH)
    for copy in id_copies + [x_copy, r_copy, wg_copy, w1_copy, w2_copy]:
        copy.start()

    expert = iota((DEVS, seq), 0)
    earlier = (iota((seq, seq), 0) < iota((seq, seq), 1)).astype(F32).astype(BF16)
    id_wait.wait()
    e1, e2, k2 = ids[0], ids[1], ids[2]
    hot1 = (e1 == expert).astype(F32)
    hot2 = (e2 == expert).astype(F32)
    kept2 = hot2 * k2.astype(F32)
    before = dot(jnp.concatenate([hot1, kept2], axis=0).astype(BF16), earlier)
    count1 = jnp.sum(hot1, axis=1, keepdims=True)
    pos1 = jnp.sum(before[:DEVS] * hot1, axis=0, keepdims=True).astype(jnp.int32)
    pos2 = jnp.sum((before[DEVS:] + count1) * hot2, axis=0, keepdims=True).astype(jnp.int32)
    keep1 = pos1 < cap
    keep2 = (pos2 < cap) & (k2 > 0)
    block1, block2 = block_of(e1, me), block_of(e2, me)
    slot1 = jnp.where(keep1, block1 * cap + pos1, -1)
    slot2 = jnp.where(keep2, block2 * cap + pos2, -1)

    half_rows = [pl.ds(c * half, half) for c in range(2)]

    def dispatch_x(c):
        slot = iota((half, seq), 0) + c * half
        table = ((slot == slot1) | (slot == slot2)).astype(F32).astype(BF16)
        disp[half_rows[c], :] = table
        xs[half_rows[c], :] = dot(table, x[...]).astype(BF16)

    def dispatch_r(c):
        rs[half_rows[c], :] = dot(disp[half_rows[c], :], r[...]).astype(BF16)

    def send_blocks(kind, c, src, dst):
        for p in halves[c]:
            remote(kind, p, blk(src, p), blk(dst, p)).start()

    x_copy.wait()
    dispatch_x(0)
    pl.semaphore_wait(barrier, DEVS - 1)
    send_blocks(SEND_X, 0, xs, xe)
    xe[pl.ds(0, cap), :] = xs[pl.ds(0, cap), :]
    r_copy.wait()
    dispatch_r(0)
    wg_copy.wait()
    logits = dot(wg[...], x[...], 1, 1)
    shifted = jnp.exp(logits - jnp.max(logits, axis=0, keepdims=True))
    prob = shifted / jnp.sum(shifted, axis=0, keepdims=True)
    gate1 = jnp.sum(prob * hot1, axis=0, keepdims=True)
    gate2 = jnp.sum(prob * hot2, axis=0, keepdims=True)
    gate_sum = gate1 + gate2
    norm1 = (gate1 / gate_sum).astype(BF16).astype(F32)
    norm2 = (gate2 / gate_sum).astype(BF16).astype(F32)
    place = iota((LANES, seq), 0)
    at1 = (place == jnp.where(keep1, pos1, -1)).astype(F32).astype(BF16)
    at2 = (place == jnp.where(keep2, pos2, -1)).astype(F32).astype(BF16)
    weights = dot((hot1 * norm1).astype(BF16), at1, 1, 1) + dot((hot2 * norm2).astype(BF16), at2, 1, 1)
    prob_sum = jnp.sum(prob, axis=1, keepdims=True)
    sub, lane = iota((DEVS, LANES), 0), iota((DEVS, LANES), 1)
    stats = where(lane == sub + cap, jnp.broadcast_to(count1, (DEVS, LANES)))
    stats += where(lane == sub + cap + DEVS, jnp.broadcast_to(prob_sum, (DEVS, LANES)))
    message = weights + jnp.sum(stats, axis=0, keepdims=True)
    for e in range(DEVS):
        msg_s[e] = message[e:e + 1]
    msg_r[0] = msg_s[me]
    for p in others:
        remote(SEND_MSG, p, msg_s.at[pl.ds(peer(p), 1)], row(msg_r, p)).start()
    send_blocks(SEND_R, 0, rs, re)
    re[pl.ds(0, cap), :] = rs[pl.ds(0, cap), :]
    dispatch_x(1)
    dispatch_r(1)
    send_blocks(SEND_X, 1, xs, xe)
    send_blocks(SEND_R, 1, rs, re)
    dispt[...] = jnp.transpose(disp[...])
    own = jnp.sum(jnp.sum(x[...].astype(F32) * r[...].astype(F32), axis=0, keepdims=True), axis=1, keepdims=True)

    wide = 512
    tiles = ff // wide
    tile = lambda n: pl.ds(n * wide, wide)
    diag = iota((half, LANES), 1) == lax.rem(iota((half, LANES), 0), cap)

    def forward(c):
        rows = half_rows[c]
        for n in range(tiles + 2):
            if n < tiles:
                pre[n % 2] = dot(xe[rows, :], w1[:, tile(n)])
            if 1 <= n <= tiles:
                m = n - 1
                v = pre[m % 2]
                sq = v * v
                root = 0.7978845608028654
                t = jnp.tanh(v * (root + root * 0.044715 * sq))
                hx = 0.5 * v
                a = (hx + hx * t).astype(BF16)
                act[rows, tile(m)] = a
                actt[tile(m), rows] = jnp.transpose(a)
                slope[rows, tile(m)] = (0.5 + 0.5 * t) + hx * (1.0 - t * t) * (root + 3.0 * root * 0.044715 * sq)
            if n >= 2:
                m = n - 2
                y = dot(act[rows, tile(m)], w2[tile(m), :])
                if m:
                    y += acc[...]
                if m < tiles - 1:
                    acc[...] = y
                else:
                    ybuf[rows, :] = y.astype(BF16)

    def cotangents(c):
        rows = half_rows[c]
        mine = range(c * HALF, (c + 1) * HALF)
        spread = jnp.concatenate([jnp.broadcast_to(msg_r[p], (cap, LANES)) for p in mine], axis=0)
        weight = jnp.sum(where(diag, spread), axis=1, keepdims=True)
        r_rows = re[rows, :].astype(F32)
        gy[rows, :] = (r_rows * weight).astype(BF16)
        dots = jnp.sum(r_rows * ybuf[rows, :].astype(F32), axis=1, keepdims=True)
        dot_mat = where(diag, jnp.broadcast_to(dots, (half, LANES)))
        for p in mine:
            q = (p - c * HALF) * cap
            (dot_s if p else dot_r)[p] = jnp.sum(dot_mat[q:q + cap], axis=0, keepdims=True)

    def slot_grads(c):
        rows = half_rows[c]
        for n in range(tiles):
            da = dot(gy[rows, :], w2[tile(n), :], 1, 1).astype(BF16).astype(F32)
            dpre[rows, tile(n)] = (da * slope[rows, tile(n)]).astype(BF16)

    def back_rows(c):
        rows = half_rows[c]
        for n in range(hidden // 256):
            cols = pl.ds(n * 256, 256)
            gxs[rows, cols] = dot(dpre[rows, :], w1[cols, :], 1, 1).astype(BF16)

    def send_dots(c):
        for p in halves[c]:
            remote(SEND_DOT, p, row(dot_s, p), row(dot_r, p)).start()

    def send_back(blocks):
        for p in blocks:
            remote(SEND_GX, p, blk(gxs, p), blk(gxb, p)).start()

    w1_copy.wait()
    w2_copy.wait()
    wait_half(SEND_X, 0, blk, xe)
    forward(0)
    wait_half(SEND_MSG, 0, row, msg_r)
    wait_half(SEND_R, 0, blk, re)
    cotangents(0)
    send_dots(0)
    slot_grads(0)
    back_rows(0)
    send_back(range(1, 4))
    gxb[pl.ds(0, cap), :] = gxs[pl.ds(0, cap), :]

    wait_half(SEND_X, 1, blk, xe)
    forward(1)
    xet[...] = jnp.transpose(xe[...])
    wait_half(SEND_MSG, 1, row, msg_r)
    wait_half(SEND_R, 1, blk, re)
    cotangents(1)
    send_dots(1)
    send_back(range(4, HALF))
    slot_grads(1)

    totals = tree_sum([msg_r[p] for p in range(DEVS)])
    spread = jnp.broadcast_to(totals, (DEVS, LANES))
    count_all = jnp.sum(where(lane == sub + cap, spread), axis=1, keepdims=True)
    prob_all = jnp.sum(where(lane == sub + cap + DEVS, spread), axis=1, keepdims=True)
    frac = count_all * (1.0 / tokens_all)
    for c in range(2):
        wait_half(SEND_DOT, c, row, dot_r)
    dots = rows_of(dot_r, range(DEVS), LANES)
    high, mid, low = split3(dots)
    hit1, hit2 = block1 == expert, block2 == expert
    find = lambda part, at, hit: jnp.sum(where(hit, dot(part, at)), axis=0, keepdims=True)
    grad1, grad2 = find(high, at1, hit1), find(high, at2, hit2)
    moe = norm1 * (grad1 + find(mid, at1, hit1) + find(low, at1, hit1))
    moe += norm2 * (grad2 + find(mid, at2, hit2) + find(low, at2, hit2))
    inv_sq = 1.0 / (gate_sum * gate_sum)
    dgate1 = (grad1 - grad2) * gate2 * inv_sq
    dgate2 = (grad2 - grad1) * gate1 * inv_sq
    dprob = dgate1 * hot1 + dgate2 * hot2 + (ALPHA * hidden * DEVS) * frac
    dlogits = prob * (dprob - jnp.sum(prob * dprob, axis=0, keepdims=True))
    grad_gate = dot(dlogits.astype(BF16), x[...])
    part = jnp.broadcast_to(own + jnp.sum(moe, axis=1, keepdims=True), (DEVS, LANES))
    reduced = jnp.concatenate([grad_gate, part], axis=1)
    for e in range(DEVS):
        red_s[e] = reduced[e:e + 1]
    red_r[0] = red_s[me]
    back_rows(1)
    for p in others:
        remote(SEND_RS, p, red_s.at[pl.ds(peer(p), 1)], row(red_r, p)).start()
    send_back(halves[1])

    @pl.loop(0, tiles, unroll=2)
    def _(n):
        cols = pl.ds(pl.multiple_of(n * wide, wide), wide)
        dw2_ref[cols, :] = dot(actt[cols, :], gy[...]).astype(BF16)

    for c in range(2):
        wait_half(SEND_RS, c, row, red_r)
    total = tree_sum([red_r[p] for p in range(DEVS)])
    row_s[0] = total[:, :hidden]
    row_r[0] = total[:, :hidden]
    for p in others:
        remote(SEND_AG, p, row(row_s, 0), row(row_r, p)).start()
    aux = DEVS * jnp.sum(frac * (prob_all * (1.0 / tokens_all)), axis=0, keepdims=True)
    loss = total[:, hidden:hidden + 1] * (1.0 / numel) + ALPHA * aux
    loss_ref[...] = jnp.broadcast_to(loss, loss_ref.shape)

    @pl.loop(0, tiles, unroll=2)
    def _(n):
        cols = pl.ds(pl.multiple_of(n * wide, wide), wide)
        dw1_ref[:, cols] = dot(xet[...], dpre[:, cols]).astype(BF16)

    dlog_pad = jnp.concatenate([dlogits, jnp.zeros((LANES - DEVS, seq), F32)], axis=0)
    gate_pad = jnp.concatenate([wg[...], jnp.zeros((LANES - DEVS, hidden), BF16)], axis=0)
    router = dot(jnp.transpose(dlog_pad).astype(BF16), gate_pad)
    acc[...] = r[...].astype(F32) + router
    for c in range(2):
        wait_half(SEND_GX, c, blk, gxb)
    gx_ref[...] = (acc[...] + dot(dispt[...], gxb[...])).astype(BF16)
    for c in range(2):
        wait_half(SEND_AG, c, row, row_r)
    gw_ref[...] = rows_of(row_r, [peer(p) for p in range(DEVS)], hidden)

    for kind, view in ((SEND_X, blk(xs, 1, 15)), (SEND_R, blk(rs, 1, 15)), (SEND_GX, blk(gxs, 1, 15)),
                       (SEND_MSG, row(msg_s, 1, 15)), (SEND_DOT, row(dot_s, 1, 15)),
                       (SEND_RS, row(red_s, 1, 15)), (SEND_AG, row(row_r, 1, 15))):
        remote(kind, 1, view, view).wait_send()


def store_kernel(loss, gx, dw1, dw2, gw, loss_out, gx_out, dw1_out, dw2_out, gw_out, sem):
    pairs = [(gx, gx_out), (gw, gw_out)]
    for big, out in ((dw1, dw1_out), (dw2, dw2_out)):
        step = big.shape[0] // 4
        pairs += [(big.at[pl.ds(i * step, step)], out.at[pl.ds(i * step, step)]) for i in range(4)]
    copies = [pltpu.make_async_copy(src, dst, sem.at[i]) for i, (src, dst) in enumerate(pairs)]
    for copy in copies:
        copy.start()
    loss_out[0, 0] = jnp.max(loss[...])
    for copy in copies:
        copy.wait()


def solution(mesh):
    def layer_body(x_loc, r_loc, w_gate, w_in_loc, w_out_loc, first_ids, second_ids, keep_ids):
        _, seq, hidden = x_loc.shape
        ff = w_in_loc.shape[2]
        cap = 2 * seq // DEVS
        slots = DEVS * cap
        anyspace = pl.BlockSpec(memory_space=pl.ANY)
        vmem = pl.BlockSpec(memory_space=pltpu.VMEM)
        results = pl.pallas_call(
            functools.partial(layer_kernel, cap),
            out_shape=(
                pltpu.VMEM((8, LANES), F32),
                pltpu.VMEM((seq, hidden), BF16),
                pltpu.VMEM((hidden, ff), BF16),
                pltpu.VMEM((ff, hidden), BF16),
                pltpu.VMEM((DEVS, hidden), F32),
            ),
            in_specs=[anyspace] * 8,
            out_specs=(vmem,) * 5,
            scratch_shapes=[
                pltpu.VMEM((seq, hidden), BF16),
                pltpu.VMEM((seq, hidden), BF16),
                pltpu.VMEM((DEVS, hidden), BF16),
                pltpu.VMEM((hidden, ff), BF16),
                pltpu.VMEM((ff, hidden), BF16),
                pltpu.VMEM((3 + PAD, 1, seq), jnp.int32),
                pltpu.VMEM((slots, seq), BF16),
                pltpu.VMEM((seq, slots), BF16),
                pltpu.VMEM((slots, hidden), BF16),
                pltpu.VMEM((slots, hidden), BF16),
                pltpu.VMEM((slots, hidden), BF16),
                pltpu.VMEM((slots, hidden), BF16),
                pltpu.VMEM((slots, hidden), BF16),
                pltpu.VMEM((2, HALF * cap, 512), F32),
                pltpu.VMEM((slots, ff), BF16),
                pltpu.VMEM((ff, slots), BF16),
                pltpu.VMEM((HALF * cap, hidden), F32),
                pltpu.VMEM((slots, ff), F32),
                pltpu.VMEM((slots, ff), BF16),
                pltpu.VMEM((slots, hidden), BF16),
                pltpu.VMEM((slots, hidden), BF16),
                pltpu.VMEM((slots, hidden), BF16),
                pltpu.VMEM((hidden, slots), BF16),
                pltpu.VMEM((DEVS + PAD, 1, LANES), F32),
                pltpu.VMEM((DEVS + PAD, 1, LANES), F32),
                pltpu.VMEM((DEVS + PAD, 1, LANES), F32),
                pltpu.VMEM((DEVS + PAD, 1, LANES), F32),
                pltpu.VMEM((DEVS + PAD, 1, hidden + LANES), F32),
                pltpu.VMEM((DEVS + PAD, 1, hidden + LANES), F32),
                pltpu.VMEM((1 + PAD, 1, hidden), F32),
                pltpu.VMEM((DEVS + PAD, 1, hidden), F32),
                pltpu.SemaphoreType.DMA((6,)),
                pltpu.SemaphoreType.DMA((7,)),
                pltpu.SemaphoreType.DMA((7, 2)),
            ],
            compiler_params=pltpu.CompilerParams(
                collective_id=0, has_side_effects=True, vmem_limit_bytes=48 * 1024 * 1024),
            name="moe_layer",
        )(x_loc[0], r_loc[0], w_gate.T, w_in_loc[0], w_out_loc[0], first_ids, second_ids, keep_ids)
        loss, gx, dw1, dw2, gw = pl.pallas_call(
            store_kernel,
            out_shape=(
                jax.ShapeDtypeStruct((1, 1), F32),
                jax.ShapeDtypeStruct((seq, hidden), BF16),
                jax.ShapeDtypeStruct((hidden, ff), BF16),
                jax.ShapeDtypeStruct((ff, hidden), BF16),
                jax.ShapeDtypeStruct((DEVS, hidden), F32),
            ),
            in_specs=[vmem] * 5,
            out_specs=(pl.BlockSpec(memory_space=pltpu.SMEM),) + (anyspace,) * 4,
            scratch_shapes=[pltpu.SemaphoreType.DMA((10,))],
            compiler_params=pltpu.CompilerParams(vmem_limit_bytes=2 * 1024 * 1024),
            name="store_results",
        )(*results)
        return loss.reshape(()), gx[None], dw1[None], dw2[None], gw.T

    row_spec = P('ep', None, None)
    id_spec = P('ep', None)
    return jax.shard_map(layer_body, mesh=mesh, in_specs=(row_spec, row_spec, P(None, None), row_spec, row_spec, id_spec, id_spec, id_spec), out_specs=(P(), row_spec, row_spec, row_spec, P(None, None)), check_vma=False)
```

time: 54.2 us -> 46.2 us (0.85)
  Pallas kernels: 53.4 us -> 45.3 us
    pallas_call x1, Pallas kernels: 49.1 us -> 40.9 us  [layer_body(): pl.pallas_call(functools.partial(layer_kernel, cap), out_shape=(pltpu.VME...]
where the time goes in v2:
time: 46.2 us; the launch traced here: 46.1 us
  Pallas kernels  45.3 us (98%)
  between operations  0.8 us (2%)
    pallas_call x1, Pallas kernels, layer_body(): pl.pallas_call(functools.partial(layer_kernel, cap), out_shape=(pltpu.VME...  40.9 us
    pallas_call x1, Pallas kernels, layer_body(): pl.pallas_call(store_kernel, out_shape=(jax.ShapeDtypeStruct((1, 1), F32)...  4.38 us

profile of v2, /device:TPU:0, one launch (start us, length us, event | category | flops | bytes accessed | tf_op | source)
XLA Modules:
  0.0 46.1 jit_solution(6623691584797093965)
XLA Ops:
  0.6 40.9 %moe_layer.1 = (f32[8,128]{1,0:T(8,128)S(1)}, bf16[256,768]{1,0:T(8,128)(2,1)S(1)}, bf16[768,3072]{1,0:T(8,128)(2,1)S(1)}, bf16[3072,768]{1,0:T(8,128)(2,1)S(1)}, f32[16,768]{1,0:T(8,128)S(1)}) custom-call(bf16[256,768]{1,0:T(8,128)(2,1)} %bitcast.12, bf16[256,768]{1,0:T(8,128)(2,1)} %bitcast.13, bf16[16,768]{1,0:T(8,128)(2,1)} %bitcast.14, ...), custom_call_target="tpu_custom_call" | custom-call | tf_op jit(solution)/shard_map/moe_layer/pallas_call | solution.py:361
  41.5 4.4 %store_results.1 = (f32[1,1]{1,0:T(1,128)}, bf16[256,768]{1,0:T(8,128)(2,1)}, bf16[768,3072]{1,0:T(8,128)(2,1)}, bf16[3072,768]{1,0:T(8,128)(2,1)}, f32[16,768]{1,0:T(8,128)}) custom-call(f32[8,128]{1,0:T(8,128)S(1)} %get-tuple-element.15.loss, bf16[256,768]{1,0:T(8,128)(2,1)S(1)} %get-tuple-element.16.gx, bf16[768,3072]{1,0:T(8,128)(2,1)S(1)} %get-tuple-element.17.dw1, ...), custom_call_target="tpu_custom_call" | custom-call | tf_op jit(solution)/shard_map/store_results/pallas_call | solution.py:412

commit v3 on v2

--- a/solution.py
+++ b/solution.py
@@ -68,8 +68,8 @@
 
 
 def layer_kernel(cap, x_hbm, r_hbm, wg_hbm, w1_hbm, w2_hbm, e1_hbm, e2_hbm, k2_hbm,
-                 loss_ref, gx_ref, dw1_ref, dw2_ref, gw_ref,
-                 x, r, wg, w1, w2, ids, disp, dispt, xs, rs, xe, re, gy, pre, act, actt, acc, slope, dpre, ybuf, gxs, gxb, xet,
+                 loss_ref, gw_ref, dw2_ref, dw1_ref, xet, dpre, dispt, gxb, base,
+                 x, r, wg, w1, w2, w1t, w2t, ids, disp, xs, rs, xe, re, gy, pre, act, actt, acc, slope, ybuf, gxs,
                  msg_s, msg_r, dot_s, dot_r, red_s, red_r, row_s, row_r,
                  local_sem, send_sem, recv_sem):
     seq, hidden = x.shape
@@ -92,6 +92,7 @@
 
     others = range(1, DEVS)
     halves = (range(1, HALF), range(HALF, DEVS))
+    orders = ((2, 4, 6, 3, 5, 7, 1), (14, 15, 8, 10, 12, 9, 11, 13))
     blk = lambda ref, p, n=1: ref.at[pl.ds(p * cap, n * cap), :]
     row = lambda ref, p, n=1: ref.at[pl.ds(p, n)]
 
@@ -140,7 +141,7 @@
         rs[half_rows[c], :] = dot(disp[half_rows[c], :], r[...]).astype(BF16)
 
     def send_blocks(kind, c, src, dst):
-        for p in halves[c]:
+        for p in orders[c]:
             remote(kind, p, blk(src, p), blk(dst, p)).start()
 
     x_copy.wait()
@@ -171,7 +172,7 @@
     for e in range(DEVS):
         msg_s[e] = message[e:e + 1]
     msg_r[0] = msg_s[me]
-    for p in others:
+    for p in orders[1] + orders[0]:
         remote(SEND_MSG, p, msg_s.at[pl.ds(peer(p), 1)], row(msg_r, p)).start()
     send_blocks(SEND_R, 0, rs, re)
     re[pl.ds(0, cap), :] = rs[pl.ds(0, cap), :]
@@ -226,20 +227,15 @@
             q = (p - c * HALF) * cap
             (dot_s if p else dot_r)[p] = jnp.sum(dot_mat[q:q + cap], axis=0, keepdims=True)
 
-    def slot_grads(c):
-        rows = half_rows[c]
+    def slot_grads(first, count):
+        rows = pl.ds(first * cap, count * cap)
         for n in range(tiles):
-            da = dot(gy[rows, :], w2[tile(n), :], 1, 1).astype(BF16).astype(F32)
+            da = dot(gy[rows, :], w2t[:, tile(n)]).astype(BF16).astype(F32)
             dpre[rows, tile(n)] = (da * slope[rows, tile(n)]).astype(BF16)
-
-    def back_rows(c):
-        rows = half_rows[c]
-        for n in range(hidden // 256):
-            cols = pl.ds(n * 256, 256)
-            gxs[rows, cols] = dot(dpre[rows, :], w1[cols, :], 1, 1).astype(BF16)
+        gxs[rows, :] = dot(dpre[rows, :], w1t[...]).astype(BF16)
 
     def send_dots(c):
-        for p in halves[c]:
+        for p in orders[c]:
             remote(SEND_DOT, p, row(dot_s, p), row(dot_r, p)).start()
 
     def send_back(blocks):
@@ -248,15 +244,21 @@
 
     w1_copy.wait()
     w2_copy.wait()
+
+    @pl.loop(0, tiles)
+    def _(n):
+        cols = pl.ds(pl.multiple_of(n * wide, wide), wide)
+        w2t[:, cols] = jnp.transpose(w2[cols, :])
+        w1t[cols, :] = jnp.transpose(w1[:, cols])
+
     wait_half(SEND_X, 0, blk, xe)
     forward(0)
     wait_half(SEND_MSG, 0, row, msg_r)
     wait_half(SEND_R, 0, blk, re)
     cotangents(0)
     send_dots(0)
-    slot_grads(0)
-    back_rows(0)
-    send_back(range(1, 4))
+    slot_grads(0, HALF)
+    send_back((2, 4, 1))
     gxb[pl.ds(0, cap), :] = gxs[pl.ds(0, cap), :]
 
     wait_half(SEND_X, 1, blk, xe)
@@ -266,8 +268,10 @@
     wait_half(SEND_R, 1, blk, re)
     cotangents(1)
     send_dots(1)
-    send_back(range(4, HALF))
-    slot_grads(1)
+    send_back((6, 3, 5, 7))
+    slot_grads(12, 4)
+    send_back((14, 15, 12, 13))
+    slot_grads(8, 4)
 
     totals = tree_sum([msg_r[p] for p in range(DEVS)])
     spread = jnp.broadcast_to(totals, (DEVS, LANES))
@@ -294,10 +298,9 @@
     for e in range(DEVS):
         red_s[e] = reduced[e:e + 1]
     red_r[0] = red_s[me]
-    back_rows(1)
-    for p in others:
+    for p in orders[1] + orders[0]:
         remote(SEND_RS, p, red_s.at[pl.ds(peer(p), 1)], row(red_r, p)).start()
-    send_back(halves[1])
+    send_back((8, 10, 9, 11))
 
     @pl.loop(0, tiles, unroll=2)
     def _(n):
@@ -309,24 +312,21 @@
     total = tree_sum([red_r[p] for p in range(DEVS)])
     row_s[0] = total[:, :hidden]
     row_r[0] = total[:, :hidden]
-    for p in others:
+    for p in orders[1] + orders[0]:
         remote(SEND_AG, p, row(row_s, 0), row(row_r, p)).start()
     aux = DEVS * jnp.sum(frac * (prob_all * (1.0 / tokens_all)), axis=0, keepdims=True)
     loss = total[:, hidden:hidden + 1] * (1.0 / numel) + ALPHA * aux
     loss_ref[...] = jnp.broadcast_to(loss, loss_ref.shape)
 
-    @pl.loop(0, tiles, unroll=2)
+    @pl.loop(0, dw1_ref.shape[0])
     def _(n):
-        cols = pl.ds(pl.multiple_of(n * wide, wide), wide)
-        dw1_ref[:, cols] = dot(xet[...], dpre[:, cols]).astype(BF16)
+        dw1_ref[n] = dot(xet[...], dpre[:, pl.ds(pl.multiple_of(n * wide, wide), wide)]).astype(BF16)
 
     dlog_pad = jnp.concatenate([dlogits, jnp.zeros((LANES - DEVS, seq), F32)], axis=0)
     gate_pad = jnp.concatenate([wg[...], jnp.zeros((LANES - DEVS, hidden), BF16)], axis=0)
-    router = dot(jnp.transpose(dlog_pad).astype(BF16), gate_pad)
-    acc[...] = r[...].astype(F32) + router
+    base[...] = r[...].astype(F32) + dot(jnp.transpose(dlog_pad).astype(BF16), gate_pad)
     for c in range(2):
         wait_half(SEND_GX, c, blk, gxb)
-    gx_ref[...] = (acc[...] + dot(dispt[...], gxb[...])).astype(BF16)
     for c in range(2):
         wait_half(SEND_AG, c, row, row_r)
     gw_ref[...] = rows_of(row_r, [peer(p) for p in range(DEVS)], hidden)
@@ -337,14 +337,21 @@
         remote(kind, 1, view, view).wait_send()
 
 
-def store_kernel(loss, gx, dw1, dw2, gw, loss_out, gx_out, dw1_out, dw2_out, gw_out, sem):
-    pairs = [(gx, gx_out), (gw, gw_out)]
-    for big, out in ((dw1, dw1_out), (dw2, dw2_out)):
-        step = big.shape[0] // 4
-        pairs += [(big.at[pl.ds(i * step, step)], out.at[pl.ds(i * step, step)]) for i in range(4)]
+def store_kernel(loss, gw, dw2, dw1, xet, dpre, dispt, gxb, base,
+                 loss_out, gx_out, dw1_out, dw2_out, gw_out, gx, tiles, sem):
+    done, _, wide = dw1.shape
+    more = tiles.shape[0]
+    tile = lambda n: pl.ds(n * wide, wide)
+    pairs = [(dw2, dw2_out), (gw, gw_out)] + [(dw1.at[n], dw1_out.at[:, tile(n)]) for n in range(done)]
+    pairs += [(tiles.at[n], dw1_out.at[:, tile(done + n)]) for n in range(more)] + [(gx, gx_out)]
     copies = [pltpu.make_async_copy(src, dst, sem.at[i]) for i, (src, dst) in enumerate(pairs)]
-    for copy in copies:
+    for copy in copies[:2 + done]:
         copy.start()
+    for n in range(more):
+        tiles[n] = dot(xet[...], dpre[:, tile(done + n)]).astype(BF16)
+        copies[2 + done + n].start()
+    gx[...] = (base[...] + dot(dispt[...], gxb[...])).astype(BF16)
+    copies[-1].start()
     loss_out[0, 0] = jnp.max(loss[...])
     for copy in copies:
         copy.wait()
@@ -358,26 +365,33 @@
         slots = DEVS * cap
         anyspace = pl.BlockSpec(memory_space=pl.ANY)
         vmem = pl.BlockSpec(memory_space=pltpu.VMEM)
+        wide, early = 512, 4
+        late = ff // wide - early
         results = pl.pallas_call(
             functools.partial(layer_kernel, cap),
             out_shape=(
                 pltpu.VMEM((8, LANES), F32),
-                pltpu.VMEM((seq, hidden), BF16),
-                pltpu.VMEM((hidden, ff), BF16),
+                pltpu.VMEM((DEVS, hidden), F32),
                 pltpu.VMEM((ff, hidden), BF16),
-                pltpu.VMEM((DEVS, hidden), F32),
+                pltpu.VMEM((early, hidden, wide), BF16),
+                pltpu.VMEM((hidden, slots), BF16),
+                pltpu.VMEM((slots, ff), BF16),
+                pltpu.VMEM((seq, slots), BF16),
+                pltpu.VMEM((slots, hidden), BF16),
+                pltpu.VMEM((seq, hidden), F32),
             ),
             in_specs=[anyspace] * 8,
-            out_specs=(vmem,) * 5,
+            out_specs=(vmem,) * 9,
             scratch_shapes=[
                 pltpu.VMEM((seq, hidden), BF16),
                 pltpu.VMEM((seq, hidden), BF16),
                 pltpu.VMEM((DEVS, hidden), BF16),
                 pltpu.VMEM((hidden, ff), BF16),
                 pltpu.VMEM((ff, hidden), BF16),
+                pltpu.VMEM((ff, hidden), BF16),
+                pltpu.VMEM((hidden, ff), BF16),
                 pltpu.VMEM((3 + PAD, 1, seq), jnp.int32),
                 pltpu.VMEM((slots, seq), BF16),
-                pltpu.VMEM((seq, slots), BF16),
                 pltpu.VMEM((slots, hidden), BF16),
                 pltpu.VMEM((slots, hidden), BF16),
                 pltpu.VMEM((slots, hidden), BF16),
@@ -388,11 +402,8 @@
                 pltpu.VMEM((ff, slots), BF16),
                 pltpu.VMEM((HALF * cap, hidden), F32),
                 pltpu.VMEM((slots, ff), F32),
-                pltpu.VMEM((slots, ff), BF16),
-                pltpu.VMEM((slots, hidden), BF16),
-                pltpu.VMEM((slots, hidden), BF16),
-                pltpu.VMEM((slots, hidden), BF16),
-                pltpu.VMEM((hidden, slots), BF16),
+                pltpu.VMEM((slots, hidden), BF16),
+                pltpu.VMEM((slots, hidden), BF16),
                 pltpu.VMEM((DEVS + PAD, 1, LANES), F32),
                 pltpu.VMEM((DEVS + PAD, 1, LANES), F32),
                 pltpu.VMEM((DEVS + PAD, 1, LANES), F32),
@@ -418,10 +429,14 @@
                 jax.ShapeDtypeStruct((ff, hidden), BF16),
                 jax.ShapeDtypeStruct((DEVS, hidden), F32),
             ),
-            in_specs=[vmem] * 5,
+            in_specs=[vmem] * 9,
             out_specs=(pl.BlockSpec(memory_space=pltpu.SMEM),) + (anyspace,) * 4,
-            scratch_shapes=[pltpu.SemaphoreType.DMA((10,))],
-            compiler_params=pltpu.CompilerParams(vmem_limit_bytes=2 * 1024 * 1024),
+            scratch_shapes=[
+                pltpu.VMEM((seq, hidden), BF16),
+                pltpu.VMEM((late, hidden, wide), BF16),
+                pltpu.SemaphoreType.DMA((3 + ff // wide,)),
+            ],
+            compiler_params=pltpu.CompilerParams(vmem_limit_bytes=12 * 1024 * 1024),
             name="store_results",
         )(*results)
         return loss.reshape(()), gx[None], dw1[None], dw2[None], gw.T

time: 46.2 us -> 44.2 us (0.957)
  Pallas kernels: 45.3 us -> 43.2 us
    pallas_call x1, Pallas kernels: 40.9 us -> 38.8 us  [layer_body(): pl.pallas_call(functools.partial(layer_kernel, cap), out_shape=(pltpu.VME...]
where the time goes in v3:
time: 44.2 us; the launch traced here: 44 us
  Pallas kernels  43.2 us (98%)
  between operations  0.8 us (2%)
    pallas_call x1, Pallas kernels, layer_body(): pl.pallas_call(functools.partial(layer_kernel, cap), out_shape=(pltpu.VME...  38.8 us
    pallas_call x1, Pallas kernels, layer_body(): pl.pallas_call(store_kernel, out_shape=(jax.ShapeDtypeStruct((1, 1), F32)...  4.45 us

profile of v3, /device:TPU:0, one launch (start us, length us, event | category | flops | bytes accessed | tf_op | source)
XLA Modules:
  0.0 44.0 jit_solution(10022824541342855801)
XLA Ops:
  0.6 38.8 %moe_layer.1 = (f32[8,128]{1,0:T(8,128)S(1)}, f32[16,768]{1,0:T(8,128)S(1)}, bf16[3072,768]{1,0:T(8,128)(2,1)S(1)}, bf16[4,768,512]{2,1,0:T(8,128)(2,1)S(1)}, bf...) custom-call(bf16[256,768]{1,0:T(8,128)(2,1)} %bitcast.12, ...), custom_call_target="tpu_custom_call" | custom-call | tf_op jit(solution)/shard_map/moe_layer/pallas_call | solution.py:370
  39.4 4.5 %store_results.1 = (f32[1,1]{1,0:T(1,128)}, bf16[256,768]{1,0:T(8,128)(2,1)}, bf16[768,3072]{1,0:T(8,128)(2,1)}, bf16[3072,768]{1,0:T(8,128)(2,1)}, f32[16,768]{1,0:T(8,128)}) custom-call(f32[8,128]{1,0:T(8,128)S(1)} %get-tuple-element.19.loss, f32[16,768]{1,0:T(8,128)S(1)} %get-tuple-element.20.gw, bf16[3072,768]{1,0:T(8,128)(2,1)S(1)} %get-tuple-element.21.dw2, ...), custom_call_target="tpu_custom_call" | custom-call | tf_op jit(solution)/shard_map/store_results/pallas_call | solution.py:423

commit v4 on v3

--- a/solution.py
+++ b/solution.py
@@ -21,15 +21,15 @@
 
 
 def offset_of(p):
-    x, y = (p >> 1) & 1, (p >> 2) & 1
-    z = x ^ y ^ ((p >> 3) & 1)
-    return (p & 1) | (x << 1) | (y << 2) | (z << 3)
+    x, y, core = p & 1, (p >> 1) & 1, (p >> 2) & 1
+    z = x ^ y ^ (p >> 3)
+    return core | (x << 1) | (y << 2) | (z << 3)
 
 
 def block_of(ids, me):
     k = jnp.bitwise_xor(ids, me)
-    parity = (k >> 1) ^ (k >> 2) ^ (k >> 3)
-    return (k & 7) + 8 * (parity & 1)
+    core, x, y, z = [(k >> i) & 1 for i in range(4)]
+    return x + 2 * y + 4 * core + 8 * (x ^ y ^ z)
 
 
 def dot(a, b, ca=1, cb=0):
@@ -92,7 +92,7 @@
 
     others = range(1, DEVS)
     halves = (range(1, HALF), range(HALF, DEVS))
-    orders = ((2, 4, 6, 3, 5, 7, 1), (14, 15, 8, 10, 12, 9, 11, 13))
+    orders = ((1, 2, 3, 5, 6, 7, 4), (11, 15, 8, 9, 10, 12, 13, 14))
     blk = lambda ref, p, n=1: ref.at[pl.ds(p * cap, n * cap), :]
     row = lambda ref, p, n=1: ref.at[pl.ds(p, n)]
 
@@ -149,6 +149,8 @@
     pl.semaphore_wait(barrier, DEVS - 1)
     send_blocks(SEND_X, 0, xs, xe)
     xe[pl.ds(0, cap), :] = xs[pl.ds(0, cap), :]
+    dispatch_x(1)
+    send_blocks(SEND_X, 1, xs, xe)
     r_copy.wait()
     dispatch_r(0)
     wg_copy.wait()
@@ -158,17 +160,28 @@
     gate1 = jnp.sum(prob * hot1, axis=0, keepdims=True)
     gate2 = jnp.sum(prob * hot2, axis=0, keepdims=True)
     gate_sum = gate1 + gate2
-    norm1 = (gate1 / gate_sum).astype(BF16).astype(F32)
-    norm2 = (gate2 / gate_sum).astype(BF16).astype(F32)
+    norm1, norm2 = gate1 / gate_sum, gate2 / gate_sum
+    gamma = norm1 * norm2
     place = iota((LANES, seq), 0)
-    at1 = (place == jnp.where(keep1, pos1, -1)).astype(F32).astype(BF16)
-    at2 = (place == jnp.where(keep2, pos2, -1)).astype(F32).astype(BF16)
-    weights = dot((hot1 * norm1).astype(BF16), at1, 1, 1) + dot((hot2 * norm2).astype(BF16), at2, 1, 1)
+
+    def by_slot(first, second, shift):
+        n = len(first)
+        total = 0.0
+        for hot, values, pos, keep in ((hot1, first, pos1, keep1), (hot2, second, pos2, keep2)):
+            table = (place == jnp.where(keep, pos + shift, -1)).astype(F32).astype(BF16)
+            stack = jnp.concatenate([hot * v.astype(F32) for v in values], axis=0).astype(BF16)
+            total += dot(stack, table, 1, 1)
+        return sum(total[i * DEVS:(i + 1) * DEVS] for i in range(n))
+
+    gamma_parts = split3(gamma)
+    message = by_slot([norm1.astype(BF16)], [norm2.astype(BF16)], 0)
+    message += by_slot(gamma_parts, gamma_parts, cap) + by_slot([e2], [e1], 2 * cap)
     prob_sum = jnp.sum(prob, axis=1, keepdims=True)
     sub, lane = iota((DEVS, LANES), 0), iota((DEVS, LANES), 1)
-    stats = where(lane == sub + cap, jnp.broadcast_to(count1, (DEVS, LANES)))
-    stats += where(lane == sub + cap + DEVS, jnp.broadcast_to(prob_sum, (DEVS, LANES)))
-    message = weights + jnp.sum(stats, axis=0, keepdims=True)
+    count_lane, prob_lane = lane == sub + 3 * cap, lane == sub + 3 * cap + DEVS
+    stats = where(count_lane, jnp.broadcast_to(count1, (DEVS, LANES)))
+    stats += where(prob_lane, jnp.broadcast_to(prob_sum, (DEVS, LANES)))
+    message += jnp.sum(stats, axis=0, keepdims=True)
     for e in range(DEVS):
         msg_s[e] = message[e:e + 1]
     msg_r[0] = msg_s[me]
@@ -176,9 +189,7 @@
         remote(SEND_MSG, p, msg_s.at[pl.ds(peer(p), 1)], row(msg_r, p)).start()
     send_blocks(SEND_R, 0, rs, re)
     re[pl.ds(0, cap), :] = rs[pl.ds(0, cap), :]
-    dispatch_x(1)
     dispatch_r(1)
-    send_blocks(SEND_X, 1, xs, xe)
     send_blocks(SEND_R, 1, rs, re)
     dispt[...] = jnp.transpose(disp[...])
     own = jnp.sum(jnp.sum(x[...].astype(F32) * r[...].astype(F32), axis=0, keepdims=True), axis=1, keepdims=True)
@@ -186,7 +197,7 @@
     wide = 512
     tiles = ff // wide
     tile = lambda n: pl.ds(n * wide, wide)
-    diag = iota((half, LANES), 1) == lax.rem(iota((half, LANES), 0), cap)
+    lane_of, slot_of = iota((half, LANES), 1), lax.rem(iota((half, LANES), 0), cap)
 
     def forward(c):
         rows = half_rows[c]
@@ -218,14 +229,19 @@
         rows = half_rows[c]
         mine = range(c * HALF, (c + 1) * HALF)
         spread = jnp.concatenate([jnp.broadcast_to(msg_r[p], (cap, LANES)) for p in mine], axis=0)
-        weight = jnp.sum(where(diag, spread), axis=1, keepdims=True)
+        column = lambda i: jnp.sum(where(lane_of == slot_of + i * cap, spread), axis=1, keepdims=True)
+        weight, scale, other = column(0), column(1), column(2)
         r_rows = re[rows, :].astype(F32)
         gy[rows, :] = (r_rows * weight).astype(BF16)
         dots = jnp.sum(r_rows * ybuf[rows, :].astype(F32), axis=1, keepdims=True)
-        dot_mat = where(diag, jnp.broadcast_to(dots, (half, LANES)))
+        dot_mat = where(lane_of == slot_of, jnp.broadcast_to(dots, (half, LANES)))
         for p in mine:
             q = (p - c * HALF) * cap
             (dot_s if p else dot_r)[p] = jnp.sum(dot_mat[q:q + cap], axis=0, keepdims=True)
+        share = jnp.broadcast_to(dots.astype(BF16).astype(F32) * scale, (half, LANES))
+        table = where(lane_of == me, share) - where(lane_of == other.astype(jnp.int32), share)
+        part = dot(jnp.transpose(table).astype(BF16), xe[rows, :])[:DEVS]
+        return part, jnp.sum(weight * dots, axis=0, keepdims=True)
 
     def slot_grads(first, count):
         rows = pl.ds(first * cap, count * cap)
@@ -251,61 +267,41 @@
         w2t[:, cols] = jnp.transpose(w2[cols, :])
         w1t[cols, :] = jnp.transpose(w1[:, cols])
 
-    wait_half(SEND_X, 0, blk, xe)
-    forward(0)
-    wait_half(SEND_MSG, 0, row, msg_r)
+    for c in range(2):
+        wait_half(SEND_X, c, blk, xe)
+        forward(c)
+    xet[...] = jnp.transpose(xe[...])
+
+    for c in range(2):
+        wait_half(SEND_MSG, c, row, msg_r)
+    totals = jnp.broadcast_to(tree_sum([msg_r[p] for p in range(DEVS)]), (DEVS, LANES))
+    frac = jnp.sum(where(count_lane, totals), axis=1, keepdims=True) * (1.0 / tokens_all)
+    mean_prob = jnp.sum(where(prob_lane, totals), axis=1, keepdims=True) * (1.0 / tokens_all)
+    aux_prob = (ALPHA * hidden * DEVS) * frac
+    aux_logits = prob * (aux_prob - jnp.sum(prob * aux_prob, axis=0, keepdims=True))
+    aux_part = dot(aux_logits.astype(BF16), x[...])
+
     wait_half(SEND_R, 0, blk, re)
-    cotangents(0)
+    part0, loss0 = cotangents(0)
+    part0 += aux_part
+    loss0 += own
     send_dots(0)
     slot_grads(0, HALF)
-    send_back((2, 4, 1))
     gxb[pl.ds(0, cap), :] = gxs[pl.ds(0, cap), :]
 
-    wait_half(SEND_X, 1, blk, xe)
-    forward(1)
-    xet[...] = jnp.transpose(xe[...])
-    wait_half(SEND_MSG, 1, row, msg_r)
     wait_half(SEND_R, 1, blk, re)
-    cotangents(1)
-    send_dots(1)
-    send_back((6, 3, 5, 7))
-    slot_grads(12, 4)
-    send_back((14, 15, 12, 13))
-    slot_grads(8, 4)
-
-    totals = tree_sum([msg_r[p] for p in range(DEVS)])
-    spread = jnp.broadcast_to(totals, (DEVS, LANES))
-    count_all = jnp.sum(where(lane == sub + cap, spread), axis=1, keepdims=True)
-    prob_all = jnp.sum(where(lane == sub + cap + DEVS, spread), axis=1, keepdims=True)
-    frac = count_all * (1.0 / tokens_all)
-    for c in range(2):
-        wait_half(SEND_DOT, c, row, dot_r)
-    dots = rows_of(dot_r, range(DEVS), LANES)
-    high, mid, low = split3(dots)
-    hit1, hit2 = block1 == expert, block2 == expert
-    find = lambda part, at, hit: jnp.sum(where(hit, dot(part, at)), axis=0, keepdims=True)
-    grad1, grad2 = find(high, at1, hit1), find(high, at2, hit2)
-    moe = norm1 * (grad1 + find(mid, at1, hit1) + find(low, at1, hit1))
-    moe += norm2 * (grad2 + find(mid, at2, hit2) + find(low, at2, hit2))
-    inv_sq = 1.0 / (gate_sum * gate_sum)
-    dgate1 = (grad1 - grad2) * gate2 * inv_sq
-    dgate2 = (grad2 - grad1) * gate1 * inv_sq
-    dprob = dgate1 * hot1 + dgate2 * hot2 + (ALPHA * hidden * DEVS) * frac
-    dlogits = prob * (dprob - jnp.sum(prob * dprob, axis=0, keepdims=True))
-    grad_gate = dot(dlogits.astype(BF16), x[...])
-    part = jnp.broadcast_to(own + jnp.sum(moe, axis=1, keepdims=True), (DEVS, LANES))
-    reduced = jnp.concatenate([grad_gate, part], axis=1)
+    part1, loss1 = cotangents(1)
+    reduced = jnp.concatenate([part0 + part1, jnp.broadcast_to(loss0 + loss1, (DEVS, LANES))], axis=1)
     for e in range(DEVS):
         red_s[e] = reduced[e:e + 1]
     red_r[0] = red_s[me]
     for p in orders[1] + orders[0]:
         remote(SEND_RS, p, red_s.at[pl.ds(peer(p), 1)], row(red_r, p)).start()
-    send_back((8, 10, 9, 11))
-
-    @pl.loop(0, tiles, unroll=2)
-    def _(n):
-        cols = pl.ds(pl.multiple_of(n * wide, wide), wide)
-        dw2_ref[cols, :] = dot(actt[cols, :], gy[...]).astype(BF16)
+    send_dots(1)
+    send_back((1, 2, 3, 5, 6, 7, 4))
+    slot_grads(8, 4)
+    send_back((11, 8, 9, 10))
+    slot_grads(12, 4)
 
     for c in range(2):
         wait_half(SEND_RS, c, row, red_r)
@@ -314,14 +310,27 @@
     row_r[0] = total[:, :hidden]
     for p in orders[1] + orders[0]:
         remote(SEND_AG, p, row(row_s, 0), row(row_r, p)).start()
-    aux = DEVS * jnp.sum(frac * (prob_all * (1.0 / tokens_all)), axis=0, keepdims=True)
+    send_back((15, 12, 13, 14))
+    aux = DEVS * jnp.sum(frac * mean_prob, axis=0, keepdims=True)
     loss = total[:, hidden:hidden + 1] * (1.0 / numel) + ALPHA * aux
     loss_ref[...] = jnp.broadcast_to(loss, loss_ref.shape)
+
+    @pl.loop(0, tiles, unroll=2)
+    def _(n):
+        cols = pl.ds(pl.multiple_of(n * wide, wide), wide)
+        dw2_ref[cols, :] = dot(actt[cols, :], gy[...]).astype(BF16)
 
     @pl.loop(0, dw1_ref.shape[0])
     def _(n):
         dw1_ref[n] = dot(xet[...], dpre[:, pl.ds(pl.multiple_of(n * wide, wide), wide)]).astype(BF16)
 
+    for c in range(2):
+        wait_half(SEND_DOT, c, row, dot_r)
+    dots = rows_of(dot_r, range(DEVS), LANES).astype(BF16)
+    at = lambda pos, keep: (place == jnp.where(keep, pos, -1)).astype(F32).astype(BF16)
+    grad1 = jnp.sum(where(block1 == expert, dot(dots, at(pos1, keep1))), axis=0, keepdims=True)
+    grad2 = jnp.sum(where(block2 == expert, dot(dots, at(pos2, keep2))), axis=0, keepdims=True)
+    dlogits = aux_logits + gamma * (grad1 - grad2) * (hot1 - hot2)
     dlog_pad = jnp.concatenate([dlogits, jnp.zeros((LANES - DEVS, seq), F32)], axis=0)
     gate_pad = jnp.concatenate([wg[...], jnp.zeros((LANES - DEVS, hidden), BF16)], axis=0)
     base[...] = r[...].astype(F32) + dot(jnp.transpose(dlog_pad).astype(BF16), gate_pad)
@@ -338,21 +347,22 @@
 
 
 def store_kernel(loss, gw, dw2, dw1, xet, dpre, dispt, gxb, base,
-                 loss_out, gx_out, dw1_out, dw2_out, gw_out, gx, tiles, sem):
+                 loss_out, gx_out, dw1_out, dw2_out, gw_out, gx, tiles, loss_buf, sem):
     done, _, wide = dw1.shape
     more = tiles.shape[0]
     tile = lambda n: pl.ds(n * wide, wide)
     pairs = [(dw2, dw2_out), (gw, gw_out)] + [(dw1.at[n], dw1_out.at[:, tile(n)]) for n in range(done)]
-    pairs += [(tiles.at[n], dw1_out.at[:, tile(done + n)]) for n in range(more)] + [(gx, gx_out)]
+    pairs += [(tiles.at[n], dw1_out.at[:, tile(done + n)]) for n in range(more)] + [(gx, gx_out), (loss_buf, loss_out)]
     copies = [pltpu.make_async_copy(src, dst, sem.at[i]) for i, (src, dst) in enumerate(pairs)]
     for copy in copies[:2 + done]:
         copy.start()
+    loss_buf[0, 0] = jnp.max(loss[...])
+    copies[-1].start()
     for n in range(more):
         tiles[n] = dot(xet[...], dpre[:, tile(done + n)]).astype(BF16)
         copies[2 + done + n].start()
     gx[...] = (base[...] + dot(dispt[...], gxb[...])).astype(BF16)
-    copies[-1].start()
-    loss_out[0, 0] = jnp.max(loss[...])
+    copies[-2].start()
     for copy in copies:
         copy.wait()
 
@@ -430,11 +440,12 @@
                 jax.ShapeDtypeStruct((DEVS, hidden), F32),
             ),
             in_specs=[vmem] * 9,
-            out_specs=(pl.BlockSpec(memory_space=pltpu.SMEM),) + (anyspace,) * 4,
+            out_specs=(anyspace,) * 5,
             scratch_shapes=[
                 pltpu.VMEM((seq, hidden), BF16),
                 pltpu.VMEM((late, hidden, wide), BF16),
-                pltpu.SemaphoreType.DMA((3 + ff // wide,)),
+                pltpu.SMEM((1, 1), F32),
+                pltpu.SemaphoreType.DMA((4 + ff // wide,)),
             ],
             compiler_params=pltpu.CompilerParams(vmem_limit_bytes=12 * 1024 * 1024),
             name="store_results",

time: 44.2 us -> 42.2 us (0.955)
  Pallas kernels: 43.2 us -> 41.3 us
    pallas_call x1, Pallas kernels: 38.8 us -> 37.4 us  [layer_body(): pl.pallas_call(functools.partial(layer_kernel, cap), out_shape=(pltpu.VME...]
    pallas_call x1, Pallas kernels: 4.45 us -> 3.84 us  [layer_body(): pl.pallas_call(store_kernel, out_shape=(jax.ShapeDtypeStruct((1, 1), F32)...]
where the time goes in v4:
time: 42.2 us; the launch traced here: 42.1 us
  Pallas kernels  41.3 us (98%)
  between operations  0.8 us (2%)
    pallas_call x1, Pallas kernels, layer_body(): pl.pallas_call(functools.partial(layer_kernel, cap), out_shape=(pltpu.VME...  37.4 us
    pallas_call x1, Pallas kernels, layer_body(): pl.pallas_call(store_kernel, out_shape=(jax.ShapeDtypeStruct((1, 1), F32)...  3.84 us

profile of v4, /device:TPU:0, one launch (start us, length us, event | category | flops | bytes accessed | tf_op | source)
XLA Modules:
  0.0 42.1 jit_solution(15709115332989928321)
XLA Ops:
  0.6 37.4 %moe_layer.1 = (f32[8,128]{1,0:T(8,128)S(1)}, f32[16,768]{1,0:T(8,128)S(1)}, bf16[3072,768]{1,0:T(8,128)(2,1)S(1)}, bf16[4,768,512]{2,1,0:T(8,128)(2,1)S(1)}, bf...) custom-call(bf16[256,768]{1,0:T(8,128)(2,1)} %bitcast.12, ...), custom_call_target="tpu_custom_call" | custom-call | tf_op jit(solution)/shard_map/moe_layer/pallas_call | solution.py:380
  38.1 3.8 %store_results.1 = (f32[1,1]{1,0:T(1,128)}, bf16[256,768]{1,0:T(8,128)(2,1)}, bf16[768,3072]{1,0:T(8,128)(2,1)}, bf16[3072,768]{1,0:T(8,128)(2,1)}, f32[16,768]{1,0:T(8,128)}) custom-call(f32[8,128]{1,0:T(8,128)S(1)} %get-tuple-element.19.loss, f32[16,768]{1,0:T(8,128)S(1)} %get-tuple-element.20.gw, bf16[3072,768]{1,0:T(8,128)(2,1)S(1)} %get-tuple-element.21.dw2, ...), custom_call_target="tpu_custom_call" | custom-call | tf_op jit(solution)/shard_map/store_results/pallas_call | solution.py:433

commit v5 on v4

--- a/solution.py
+++ b/solution.py
@@ -15,7 +15,7 @@
 DEVS = 16
 LANES = 128
 PAD = 8
-HALF = 8
+PART = 4
 
 SEND_X, SEND_R, SEND_MSG, SEND_DOT, SEND_GX, SEND_RS, SEND_AG = range(7)
 
@@ -74,7 +74,8 @@
                  local_sem, send_sem, recv_sem):
     seq, hidden = x.shape
     ff = w1.shape[1]
-    half = HALF * cap
+    part_rows = PART * cap
+    parts = range(DEVS // PART)
     tokens_all = DEVS * seq
     numel = tokens_all * hidden
 
@@ -87,19 +88,22 @@
 
     def remote(kind, p, src, dst):
         return pltpu.make_async_remote_copy(
-            src_ref=src, dst_ref=dst, send_sem=send_sem.at[kind], recv_sem=recv_sem.at[kind, p // HALF],
+            src_ref=src, dst_ref=dst, send_sem=send_sem.at[kind], recv_sem=recv_sem.at[kind, p // PART],
             device_id=(peer(p),), device_id_type=MESH)
 
     others = range(1, DEVS)
-    halves = (range(1, HALF), range(HALF, DEVS))
-    orders = ((1, 2, 3, 5, 6, 7, 4), (11, 15, 8, 9, 10, 12, 13, 14))
+    orders = ((1, 2, 3), (5, 6, 7, 4), (11, 8, 9, 10), (15, 12, 13, 14))
+    far_first = orders[3] + orders[2] + orders[1] + orders[0]
     blk = lambda ref, p, n=1: ref.at[pl.ds(p * cap, n * cap), :]
     row = lambda ref, p, n=1: ref.at[pl.ds(p, n)]
 
-    def wait_half(kind, c, part, ref):
-        first, count = halves[c][0], len(halves[c])
-        view = part(ref, first, count)
-        remote(kind, first, view, view).wait_recv()
+    def wait_part(kind, c, part, ref):
+        view = part(ref, min(orders[c]), len(orders[c]))
+        remote(kind, orders[c][0], view, view).wait_recv()
+
+    def wait_all(kind, part, ref):
+        for c in parts:
+            wait_part(kind, c, part, ref)
 
     id_copies = [pltpu.make_async_copy(src, ids.at[i], local_sem.at[0]) for i, src in enumerate((e1_hbm, e2_hbm, k2_hbm))]
     id_wait = pltpu.make_async_copy(row(ids, 0, 3), row(ids, 0, 3), local_sem.at[0])
@@ -129,16 +133,16 @@
     slot1 = jnp.where(keep1, block1 * cap + pos1, -1)
     slot2 = jnp.where(keep2, block2 * cap + pos2, -1)
 
-    half_rows = [pl.ds(c * half, half) for c in range(2)]
+    rows_in = [pl.ds(c * part_rows, part_rows) for c in parts]
 
     def dispatch_x(c):
-        slot = iota((half, seq), 0) + c * half
+        slot = iota((part_rows, seq), 0) + c * part_rows
         table = ((slot == slot1) | (slot == slot2)).astype(F32).astype(BF16)
-        disp[half_rows[c], :] = table
-        xs[half_rows[c], :] = dot(table, x[...]).astype(BF16)
+        disp[rows_in[c], :] = table
+        xs[rows_in[c], :] = dot(table, x[...]).astype(BF16)
 
     def dispatch_r(c):
-        rs[half_rows[c], :] = dot(disp[half_rows[c], :], r[...]).astype(BF16)
+        rs[rows_in[c], :] = dot(disp[rows_in[c], :], r[...]).astype(BF16)
 
     def send_blocks(kind, c, src, dst):
         for p in orders[c]:
@@ -185,25 +189,35 @@
     for e in range(DEVS):
         msg_s[e] = message[e:e + 1]
     msg_r[0] = msg_s[me]
-    for p in orders[1] + orders[0]:
+    for p in far_first:
         remote(SEND_MSG, p, msg_s.at[pl.ds(peer(p), 1)], row(msg_r, p)).start()
     send_blocks(SEND_R, 0, rs, re)
     re[pl.ds(0, cap), :] = rs[pl.ds(0, cap), :]
-    dispatch_r(1)
-    send_blocks(SEND_R, 1, rs, re)
+    for c in (1, 2):
+        dispatch_x(c + 1)
+        send_blocks(SEND_X, c + 1, xs, xe)
+        dispatch_r(c)
+        send_blocks(SEND_R, c, rs, re)
+    dispatch_r(3)
+    send_blocks(SEND_R, 3, rs, re)
     dispt[...] = jnp.transpose(disp[...])
     own = jnp.sum(jnp.sum(x[...].astype(F32) * r[...].astype(F32), axis=0, keepdims=True), axis=1, keepdims=True)
 
     wide = 512
     tiles = ff // wide
     tile = lambda n: pl.ds(n * wide, wide)
-    lane_of, slot_of = iota((half, LANES), 1), lax.rem(iota((half, LANES), 0), cap)
+    lane_of, slot_of = iota((part_rows, LANES), 1), lax.rem(iota((part_rows, LANES), 0), cap)
 
     def forward(c):
-        rows = half_rows[c]
+        rows = rows_in[c]
+        xet[:, rows] = jnp.transpose(xe[rows, :])
         for n in range(tiles + 2):
             if n < tiles:
                 pre[n % 2] = dot(xe[rows, :], w1[:, tile(n)])
+                if c == 0:
+                    w2t[:, tile(n)] = jnp.transpose(w2[tile(n), :])
+                elif c == 1:
+                    w1t[tile(n), :] = jnp.transpose(w1[:, tile(n)])
             if 1 <= n <= tiles:
                 m = n - 1
                 v = pre[m % 2]
@@ -226,25 +240,25 @@
                     ybuf[rows, :] = y.astype(BF16)
 
     def cotangents(c):
-        rows = half_rows[c]
-        mine = range(c * HALF, (c + 1) * HALF)
+        rows = rows_in[c]
+        mine = range(c * PART, (c + 1) * PART)
         spread = jnp.concatenate([jnp.broadcast_to(msg_r[p], (cap, LANES)) for p in mine], axis=0)
         column = lambda i: jnp.sum(where(lane_of == slot_of + i * cap, spread), axis=1, keepdims=True)
         weight, scale, other = column(0), column(1), column(2)
         r_rows = re[rows, :].astype(F32)
         gy[rows, :] = (r_rows * weight).astype(BF16)
         dots = jnp.sum(r_rows * ybuf[rows, :].astype(F32), axis=1, keepdims=True)
-        dot_mat = where(lane_of == slot_of, jnp.broadcast_to(dots, (half, LANES)))
+        dot_mat = where(lane_of == slot_of, jnp.broadcast_to(dots, (part_rows, LANES)))
         for p in mine:
-            q = (p - c * HALF) * cap
+            q = (p - c * PART) * cap
             (dot_s if p else dot_r)[p] = jnp.sum(dot_mat[q:q + cap], axis=0, keepdims=True)
-        share = jnp.broadcast_to(dots.astype(BF16).astype(F32) * scale, (half, LANES))
+        share = jnp.broadcast_to(dots.astype(BF16).astype(F32) * scale, (part_rows, LANES))
         table = where(lane_of == me, share) - where(lane_of == other.astype(jnp.int32), share)
         part = dot(jnp.transpose(table).astype(BF16), xe[rows, :])[:DEVS]
         return part, jnp.sum(weight * dots, axis=0, keepdims=True)
 
-    def slot_grads(first, count):
-        rows = pl.ds(first * cap, count * cap)
+    def slot_grads(c):
+        rows = rows_in[c]
         for n in range(tiles):
             da = dot(gy[rows, :], w2t[:, tile(n)]).astype(BF16).astype(F32)
             dpre[rows, tile(n)] = (da * slope[rows, tile(n)]).astype(BF16)
@@ -254,78 +268,77 @@
         for p in orders[c]:
             remote(SEND_DOT, p, row(dot_s, p), row(dot_r, p)).start()
 
-    def send_back(blocks):
-        for p in blocks:
-            remote(SEND_GX, p, blk(gxs, p), blk(gxb, p)).start()
-
     w1_copy.wait()
     w2_copy.wait()
 
-    @pl.loop(0, tiles)
-    def _(n):
+    def forward_part(c):
+        wait_part(SEND_X, c, blk, xe)
+        forward(c)
+
+    def router_aux():
+        wait_all(SEND_MSG, row, msg_r)
+        totals = jnp.broadcast_to(tree_sum([msg_r[p] for p in range(DEVS)]), (DEVS, LANES))
+        frac = jnp.sum(where(count_lane, totals), axis=1, keepdims=True) * (1.0 / tokens_all)
+        mean_prob = jnp.sum(where(prob_lane, totals), axis=1, keepdims=True) * (1.0 / tokens_all)
+        aux_prob = (ALPHA * hidden * DEVS) * frac
+        aux_logits = prob * (aux_prob - jnp.sum(prob * aux_prob, axis=0, keepdims=True))
+        return frac, mean_prob, aux_logits
+
+    def backward_part(c, gate_part, loss_part):
+        wait_part(SEND_R, c, blk, re)
+        gate_c, loss_c = cotangents(c)
+        gate_part, loss_part = gate_part + gate_c, loss_part + loss_c
+        if c == 3:
+            reduced = jnp.concatenate([gate_part, jnp.broadcast_to(loss_part, (DEVS, LANES))], axis=1)
+            for e in range(DEVS):
+                red_s[e] = reduced[e:e + 1]
+            red_r[0] = red_s[me]
+            for p in far_first:
+                remote(SEND_RS, p, red_s.at[pl.ds(peer(p), 1)], row(red_r, p)).start()
+            send_dots(c)
+            send_blocks(SEND_GX, 2, gxs, gxb)
+        slot_grads(c)
+        if c == 0:
+            gxb[pl.ds(0, cap), :] = gxs[pl.ds(0, cap), :]
+        if c != 2:
+            send_blocks(SEND_GX, c, gxs, gxb)
+        if c != 3:
+            send_dots(c)
+        return gate_part, loss_part
+
+    forward_part(0)
+    forward_part(1)
+    frac, mean_prob, aux_logits = router_aux()
+    sums = dot(aux_logits.astype(BF16), x[...]), own
+    sums = backward_part(0, *sums)
+    for c in (1, 2):
+        forward_part(c + 1)
+        sums = backward_part(c, *sums)
+    backward_part(3, *sums)
+
+    def grad_w2(n):
         cols = pl.ds(pl.multiple_of(n * wide, wide), wide)
-        w2t[:, cols] = jnp.transpose(w2[cols, :])
-        w1t[cols, :] = jnp.transpose(w1[:, cols])
-
-    for c in range(2):
-        wait_half(SEND_X, c, blk, xe)
-        forward(c)
-    xet[...] = jnp.transpose(xe[...])
-
-    for c in range(2):
-        wait_half(SEND_MSG, c, row, msg_r)
-    totals = jnp.broadcast_to(tree_sum([msg_r[p] for p in range(DEVS)]), (DEVS, LANES))
-    frac = jnp.sum(where(count_lane, totals), axis=1, keepdims=True) * (1.0 / tokens_all)
-    mean_prob = jnp.sum(where(prob_lane, totals), axis=1, keepdims=True) * (1.0 / tokens_all)
-    aux_prob = (ALPHA * hidden * DEVS) * frac
-    aux_logits = prob * (aux_prob - jnp.sum(prob * aux_prob, axis=0, keepdims=True))
-    aux_part = dot(aux_logits.astype(BF16), x[...])
-
-    wait_half(SEND_R, 0, blk, re)
-    part0, loss0 = cotangents(0)
-    part0 += aux_part
-    loss0 += own
-    send_dots(0)
-    slot_grads(0, HALF)
-    gxb[pl.ds(0, cap), :] = gxs[pl.ds(0, cap), :]
-
-    wait_half(SEND_R, 1, blk, re)
-    part1, loss1 = cotangents(1)
-    reduced = jnp.concatenate([part0 + part1, jnp.broadcast_to(loss0 + loss1, (DEVS, LANES))], axis=1)
-    for e in range(DEVS):
-        red_s[e] = reduced[e:e + 1]
-    red_r[0] = red_s[me]
-    for p in orders[1] + orders[0]:
-        remote(SEND_RS, p, red_s.at[pl.ds(peer(p), 1)], row(red_r, p)).start()
-    send_dots(1)
-    send_back((1, 2, 3, 5, 6, 7, 4))
-    slot_grads(8, 4)
-    send_back((11, 8, 9, 10))
-    slot_grads(12, 4)
-
-    for c in range(2):
-        wait_half(SEND_RS, c, row, red_r)
+        dw2_ref[cols, :] = dot(actt[cols, :], gy[...]).astype(BF16)
+
+    pl.loop(0, 4, unroll=2)(grad_w2)
+
+    wait_all(SEND_RS, row, red_r)
     total = tree_sum([red_r[p] for p in range(DEVS)])
     row_s[0] = total[:, :hidden]
     row_r[0] = total[:, :hidden]
-    for p in orders[1] + orders[0]:
+    for p in far_first:
         remote(SEND_AG, p, row(row_s, 0), row(row_r, p)).start()
-    send_back((15, 12, 13, 14))
     aux = DEVS * jnp.sum(frac * mean_prob, axis=0, keepdims=True)
     loss = total[:, hidden:hidden + 1] * (1.0 / numel) + ALPHA * aux
     loss_ref[...] = jnp.broadcast_to(loss, loss_ref.shape)
 
-    @pl.loop(0, tiles, unroll=2)
-    def _(n):
-        cols = pl.ds(pl.multiple_of(n * wide, wide), wide)
-        dw2_ref[cols, :] = dot(actt[cols, :], gy[...]).astype(BF16)
+    pl.loop(4, tiles, unroll=2)(grad_w2)
 
     @pl.loop(0, dw1_ref.shape[0])
     def _(n):
         dw1_ref[n] = dot(xet[...], dpre[:, pl.ds(pl.multiple_of(n * wide, wide), wide)]).astype(BF16)
 
-    for c in range(2):
-        wait_half(SEND_DOT, c, row, dot_r)
+    wait_all(SEND_DOT, row, dot_r)
     dots = rows_of(dot_r, range(DEVS), LANES).astype(BF16)
     at = lambda pos, keep: (place == jnp.where(keep, pos, -1)).astype(F32).astype(BF16)
     grad1 = jnp.sum(where(block1 == expert, dot(dots, at(pos1, keep1))), axis=0, keepdims=True)
@@ -334,10 +347,8 @@
     dlog_pad = jnp.concatenate([dlogits, jnp.zeros((LANES - DEVS, seq), F32)], axis=0)
     gate_pad = jnp.concatenate([wg[...], jnp.zeros((LANES - DEVS, hidden), BF16)], axis=0)
     base[...] = r[...].astype(F32) + dot(jnp.transpose(dlog_pad).astype(BF16), gate_pad)
-    for c in range(2):
-        wait_half(SEND_GX, c, blk, gxb)
-    for c in range(2):
-        wait_half(SEND_AG, c, row, row_r)
+    wait_all(SEND_GX, blk, gxb)
+    wait_all(SEND_AG, row, row_r)
     gw_ref[...] = rows_of(row_r, [peer(p) for p in range(DEVS)], hidden)
 
     for kind, view in ((SEND_X, blk(xs, 1, 15)), (SEND_R, blk(rs, 1, 15)), (SEND_GX, blk(gxs, 1, 15)),
@@ -375,7 +386,7 @@
         slots = DEVS * cap
         anyspace = pl.BlockSpec(memory_space=pl.ANY)
         vmem = pl.BlockSpec(memory_space=pltpu.VMEM)
-        wide, early = 512, 4
+        wide, early = 512, 2
         late = ff // wide - early
         results = pl.pallas_call(
             functools.partial(layer_kernel, cap),
@@ -407,10 +418,10 @@
                 pltpu.VMEM((slots, hidden), BF16),
                 pltpu.VMEM((slots, hidden), BF16),
                 pltpu.VMEM((slots, hidden), BF16),
-                pltpu.VMEM((2, HALF * cap, 512), F32),
+                pltpu.VMEM((2, PART * cap, 512), F32),
                 pltpu.VMEM((slots, ff), BF16),
                 pltpu.VMEM((ff, slots), BF16),
-                pltpu.VMEM((HALF * cap, hidden), F32),
+                pltpu.VMEM((PART * cap, hidden), F32),
                 pltpu.VMEM((slots, ff), F32),
                 pltpu.VMEM((slots, hidden), BF16),
                 pltpu.VMEM((slots, hidden), BF16),
@@ -424,7 +435,7 @@
                 pltpu.VMEM((DEVS + PAD, 1, hidden), F32),
                 pltpu.SemaphoreType.DMA((6,)),
                 pltpu.SemaphoreType.DMA((7,)),
-                pltpu.SemaphoreType.DMA((7, 2)),
+                pltpu.SemaphoreType.DMA((7, DEVS // PART)),
             ],
             compiler_params=pltpu.CompilerParams(
                 collective_id=0, has_side_effects=True, vmem_limit_bytes=48 * 1024 * 1024),

time: 42.2 us -> 40.2 us (0.953)
  Pallas kernels: 41.3 us -> 39.3 us
    pallas_call x1, Pallas kernels: 37.4 us -> 35.4 us  [layer_body(): pl.pallas_call(functools.partial(layer_kernel, cap), out_shape=(pltpu.VME...]
where the time goes in v5:
time: 40.2 us; the launch traced here: 40.1 us
  Pallas kernels  39.3 us (98%)
  between operations  0.8 us (2%)
    pallas_call x1, Pallas kernels, layer_body(): pl.pallas_call(functools.partial(layer_kernel, cap), out_shape=(pltpu.VME...  35.4 us
    pallas_call x1, Pallas kernels, layer_body(): pl.pallas_call(store_kernel, out_shape=(jax.ShapeDtypeStruct((1, 1), F32)...  3.84 us

profile of v5, /device:TPU:0, one launch (start us, length us, event | category | flops | bytes accessed | tf_op | source)
XLA Modules:
  0.0 40.1 jit_solution(5667973132288054560)
XLA Ops:
  0.6 35.4 %moe_layer.1 = (f32[8,128]{1,0:T(8,128)S(1)}, f32[16,768]{1,0:T(8,128)S(1)}, bf16[3072,768]{1,0:T(8,128)(2,1)S(1)}, bf16[2,768,512]{2,1,0:T(8,128)(2,1)S(1)}, bf...) custom-call(bf16[256,768]{1,0:T(8,128)(2,1)} %bitcast.12, ...), custom_call_target="tpu_custom_call" | custom-call | tf_op jit(solution)/shard_map/moe_layer/pallas_call | solution.py:391
  36.1 3.8 %store_results.1 = (f32[1,1]{1,0:T(1,128)}, bf16[256,768]{1,0:T(8,128)(2,1)}, bf16[768,3072]{1,0:T(8,128)(2,1)}, bf16[3072,768]{1,0:T(8,128)(2,1)}, f32[16,768]{1,0:T(8,128)}) custom-call(f32[8,128]{1,0:T(8,128)S(1)} %get-tuple-element.19.loss, f32[16,768]{1,0:T(8,128)S(1)} %get-tuple-element.20.gw, bf16[3072,768]{1,0:T(8,128)(2,1)S(1)} %get-tuple-element.21.dw2, ...), custom_call_target="tpu_custom_call" | custom-call | tf_op jit(solution)/shard_map/store_results/pallas_call | solution.py:444

commit v6 on v5

--- a/solution.py
+++ b/solution.py
@@ -70,7 +70,7 @@
 def layer_kernel(cap, x_hbm, r_hbm, wg_hbm, w1_hbm, w2_hbm, e1_hbm, e2_hbm, k2_hbm,
                  loss_ref, gw_ref, dw2_ref, dw1_ref, xet, dpre, dispt, gxb, base,
                  x, r, wg, w1, w2, w1t, w2t, ids, disp, xs, rs, xe, re, gy, pre, act, actt, acc, slope, ybuf, gxs,
-                 msg_s, msg_r, dot_s, dot_r, red_s, red_r, row_s, row_r,
+                 msg_s, msg_r, dot_s, dot_r, red_s, red_r, row_s, row_r, held, at, ahead, gate_sums, sum_ref,
                  local_sem, send_sem, recv_sem):
     seq, hidden = x.shape
     ff = w1.shape[1]
@@ -180,6 +180,12 @@
     gamma_parts = split3(gamma)
     message = by_slot([norm1.astype(BF16)], [norm2.astype(BF16)], 0)
     message += by_slot(gamma_parts, gamma_parts, cap) + by_slot([e2], [e1], 2 * cap)
+    held[0] = prob
+    held[1] = gamma * (hot1 - hot2)
+    held[2] = (block1 == expert).astype(F32)
+    held[3] = (block2 == expert).astype(F32)
+    at[0] = (place == jnp.where(keep1, pos1, -1)).astype(F32).astype(BF16)
+    at[1] = (place == jnp.where(keep2, pos2, -1)).astype(F32).astype(BF16)
     prob_sum = jnp.sum(prob, axis=1, keepdims=True)
     sub, lane = iota((DEVS, LANES), 0), iota((DEVS, LANES), 1)
     count_lane, prob_lane = lane == sub + 3 * cap, lane == sub + 3 * cap + DEVS
@@ -202,11 +208,12 @@
     send_blocks(SEND_R, 3, rs, re)
     dispt[...] = jnp.transpose(disp[...])
     own = jnp.sum(jnp.sum(x[...].astype(F32) * r[...].astype(F32), axis=0, keepdims=True), axis=1, keepdims=True)
+    sum_ref[...] = jnp.broadcast_to(own, sum_ref.shape)
 
     wide = 512
     tiles = ff // wide
     tile = lambda n: pl.ds(n * wide, wide)
-    lane_of, slot_of = iota((part_rows, LANES), 1), lax.rem(iota((part_rows, LANES), 0), cap)
+    ahead[...] = iota((part_rows, LANES), 1) - lax.rem(iota((part_rows, LANES), 0), cap)
 
     def forward(c):
         rows = rows_in[c]
@@ -243,19 +250,20 @@
         rows = rows_in[c]
         mine = range(c * PART, (c + 1) * PART)
         spread = jnp.concatenate([jnp.broadcast_to(msg_r[p], (cap, LANES)) for p in mine], axis=0)
-        column = lambda i: jnp.sum(where(lane_of == slot_of + i * cap, spread), axis=1, keepdims=True)
+        lane_of = iota((part_rows, LANES), 1)
+        column = lambda i: jnp.sum(where(ahead[...] == i * cap, spread), axis=1, keepdims=True)
         weight, scale, other = column(0), column(1), column(2)
         r_rows = re[rows, :].astype(F32)
         gy[rows, :] = (r_rows * weight).astype(BF16)
         dots = jnp.sum(r_rows * ybuf[rows, :].astype(F32), axis=1, keepdims=True)
-        dot_mat = where(lane_of == slot_of, jnp.broadcast_to(dots, (part_rows, LANES)))
+        dot_mat = where(ahead[...] == 0, jnp.broadcast_to(dots, (part_rows, LANES)))
         for p in mine:
             q = (p - c * PART) * cap
             (dot_s if p else dot_r)[p] = jnp.sum(dot_mat[q:q + cap], axis=0, keepdims=True)
         share = jnp.broadcast_to(dots.astype(BF16).astype(F32) * scale, (part_rows, LANES))
         table = where(lane_of == me, share) - where(lane_of == other.astype(jnp.int32), share)
-        part = dot(jnp.transpose(table).astype(BF16), xe[rows, :])[:DEVS]
-        return part, jnp.sum(weight * dots, axis=0, keepdims=True)
+        gate_sums[...] += dot(jnp.transpose(table).astype(BF16), xe[rows, :])[:DEVS]
+        sum_ref[...] += jnp.broadcast_to(jnp.sum(weight * dots, axis=0, keepdims=True), sum_ref.shape)
 
     def slot_grads(c):
         rows = rows_in[c]
@@ -277,44 +285,53 @@
 
     def router_aux():
         wait_all(SEND_MSG, row, msg_r)
+        sub, lane = iota((DEVS, LANES), 0), iota((DEVS, LANES), 1)
         totals = jnp.broadcast_to(tree_sum([msg_r[p] for p in range(DEVS)]), (DEVS, LANES))
-        frac = jnp.sum(where(count_lane, totals), axis=1, keepdims=True) * (1.0 / tokens_all)
-        mean_prob = jnp.sum(where(prob_lane, totals), axis=1, keepdims=True) * (1.0 / tokens_all)
+        mean = lambda i: jnp.sum(where(lane == sub + i, totals), axis=1, keepdims=True) * (1.0 / tokens_all)
+        frac, mean_prob = mean(3 * cap), mean(3 * cap + DEVS)
+        aux = DEVS * jnp.sum(frac * mean_prob, axis=0, keepdims=True)
+        loss_ref[...] = jnp.broadcast_to(ALPHA * aux, loss_ref.shape)
         aux_prob = (ALPHA * hidden * DEVS) * frac
+        prob = held[0]
         aux_logits = prob * (aux_prob - jnp.sum(prob * aux_prob, axis=0, keepdims=True))
-        return frac, mean_prob, aux_logits
-
-    def backward_part(c, gate_part, loss_part):
+        held[0] = aux_logits
+        gate_sums[...] = dot(aux_logits.astype(BF16), x[...])
+
+    def take_rows(c):
         wait_part(SEND_R, c, blk, re)
-        gate_c, loss_c = cotangents(c)
-        gate_part, loss_part = gate_part + gate_c, loss_part + loss_c
-        if c == 3:
-            reduced = jnp.concatenate([gate_part, jnp.broadcast_to(loss_part, (DEVS, LANES))], axis=1)
-            for e in range(DEVS):
-                red_s[e] = reduced[e:e + 1]
-            red_r[0] = red_s[me]
-            for p in far_first:
-                remote(SEND_RS, p, red_s.at[pl.ds(peer(p), 1)], row(red_r, p)).start()
-            send_dots(c)
-            send_blocks(SEND_GX, 2, gxs, gxb)
-        slot_grads(c)
-        if c == 0:
-            gxb[pl.ds(0, cap), :] = gxs[pl.ds(0, cap), :]
-        if c != 2:
-            send_blocks(SEND_GX, c, gxs, gxb)
-        if c != 3:
-            send_dots(c)
-        return gate_part, loss_part
+        cotangents(c)
+
+    def send_sums():
+        reduced = jnp.concatenate([gate_sums[...], jnp.broadcast_to(sum_ref[0:1], (DEVS, LANES))], axis=1)
+        for e in range(DEVS):
+            red_s[e] = reduced[e:e + 1]
+        red_r[0] = red_s[me]
+        for p in far_first:
+            remote(SEND_RS, p, red_s.at[pl.ds(peer(p), 1)], row(red_r, p)).start()
 
     forward_part(0)
     forward_part(1)
-    frac, mean_prob, aux_logits = router_aux()
-    sums = dot(aux_logits.astype(BF16), x[...]), own
-    sums = backward_part(0, *sums)
-    for c in (1, 2):
-        forward_part(c + 1)
-        sums = backward_part(c, *sums)
-    backward_part(3, *sums)
+    router_aux()
+    take_rows(0)
+    slot_grads(0)
+    send_blocks(SEND_GX, 0, gxs, gxb)
+    gxb[pl.ds(0, cap), :] = gxs[pl.ds(0, cap), :]
+    send_dots(0)
+    forward_part(2)
+    take_rows(1)
+    slot_grads(1)
+    send_blocks(SEND_GX, 1, gxs, gxb)
+    send_dots(1)
+    forward_part(3)
+    take_rows(2)
+    take_rows(3)
+    send_sums()
+    send_dots(2)
+    send_dots(3)
+    slot_grads(2)
+    send_blocks(SEND_GX, 2, gxs, gxb)
+    slot_grads(3)
+    send_blocks(SEND_GX, 3, gxs, gxb)
 
     def grad_w2(n):
         cols = pl.ds(pl.multiple_of(n * wide, wide), wide)
@@ -328,9 +345,7 @@
     row_r[0] = total[:, :hidden]
     for p in far_first:
         remote(SEND_AG, p, row(row_s, 0), row(row_r, p)).start()
-    aux = DEVS * jnp.sum(frac * mean_prob, axis=0, keepdims=True)
-    loss = total[:, hidden:hidden + 1] * (1.0 / numel) + ALPHA * aux
-    loss_ref[...] = jnp.broadcast_to(loss, loss_ref.shape)
+    loss_ref[...] += jnp.broadcast_to(total[:, hidden:hidden + 1] * (1.0 / numel), loss_ref.shape)
 
     pl.loop(4, tiles, unroll=2)(grad_w2)
 
@@ -340,10 +355,9 @@
 
     wait_all(SEND_DOT, row, dot_r)
     dots = rows_of(dot_r, range(DEVS), LANES).astype(BF16)
-    at = lambda pos, keep: (place == jnp.where(keep, pos, -1)).astype(F32).astype(BF16)
-    grad1 = jnp.sum(where(block1 == expert, dot(dots, at(pos1, keep1))), axis=0, keepdims=True)
-    grad2 = jnp.sum(where(block2 == expert, dot(dots, at(pos2, keep2))), axis=0, keepdims=True)
-    dlogits = aux_logits + gamma * (grad1 - grad2) * (hot1 - hot2)
+    grad1 = jnp.sum(held[2] * dot(dots, at[0]), axis=0, keepdims=True)
+    grad2 = jnp.sum(held[3] * dot(dots, at[1]), axis=0, keepdims=True)
+    dlogits = held[0] + held[1] * (grad1 - grad2)
     dlog_pad = jnp.concatenate([dlogits, jnp.zeros((LANES - DEVS, seq), F32)], axis=0)
     gate_pad = jnp.concatenate([wg[...], jnp.zeros((LANES - DEVS, hidden), BF16)], axis=0)
     base[...] = r[...].astype(F32) + dot(jnp.transpose(dlog_pad).astype(BF16), gate_pad)
@@ -433,6 +447,11 @@
                 pltpu.VMEM((DEVS + PAD, 1, hidden + LANES), F32),
                 pltpu.VMEM((1 + PAD, 1, hidden), F32),
                 pltpu.VMEM((DEVS + PAD, 1, hidden), F32),
+                pltpu.VMEM((4, DEVS, seq), F32),
+                pltpu.VMEM((2, LANES, seq), BF16),
+                pltpu.VMEM((slots // DEVS * PART, LANES), jnp.int32),
+                pltpu.VMEM((DEVS, hidden), F32),
+                pltpu.VMEM((8, LANES), F32),
                 pltpu.SemaphoreType.DMA((6,)),
                 pltpu.SemaphoreType.DMA((7,)),
                 pltpu.SemaphoreType.DMA((7, DEVS // PART)),

time: 40.2 us -> 40.1 us (level)
  no operation moved by 1% of the time
where the time goes in v6:
time: 40.1 us; the launch traced here: 40 us
  Pallas kernels  39.2 us (98%)
  between operations  0.8 us (2%)
    pallas_call x1, Pallas kernels, layer_body(): pl.pallas_call(functools.partial(layer_kernel, cap), out_shape=(pltpu.VME...  35.4 us
    pallas_call x1, Pallas kernels, layer_body(): pl.pallas_call(store_kernel, out_shape=(jax.ShapeDtypeStruct((1, 1), F32)...  3.84 us

profile of v6, /device:TPU:0, one launch (start us, length us, event | category | flops | bytes accessed | tf_op | source)
XLA Modules:
  0.0 40.0 jit_solution(9243994310553167125)
XLA Ops:
  0.6 35.4 %moe_layer.1 = (f32[8,128]{1,0:T(8,128)S(1)}, f32[16,768]{1,0:T(8,128)S(1)}, bf16[3072,768]{1,0:T(8,128)(2,1)S(1)}, bf16[2,768,512]{2,1,0:T(8,128)(2,1)S(1)}, bf...) custom-call(bf16[256,768]{1,0:T(8,128)(2,1)} %bitcast.12, ...), custom_call_target="tpu_custom_call" | custom-call | tf_op jit(solution)/shard_map/moe_layer/pallas_call | solution.py:405
  36.0 3.8 %store_results.1 = (f32[1,1]{1,0:T(1,128)}, bf16[256,768]{1,0:T(8,128)(2,1)}, bf16[768,3072]{1,0:T(8,128)(2,1)}, bf16[3072,768]{1,0:T(8,128)(2,1)}, f32[16,768]{1,0:T(8,128)}) custom-call(f32[8,128]{1,0:T(8,128)S(1)} %get-tuple-element.19.loss, f32[16,768]{1,0:T(8,128)S(1)} %get-tuple-element.20.gw, bf16[3072,768]{1,0:T(8,128)(2,1)S(1)} %get-tuple-element.21.dw2, ...), custom_call_target="tpu_custom_call" | custom-call | tf_op jit(solution)/shard_map/store_results/pallas_call | solution.py:463
